TPU v7x, 32 devices: a whole 2x2x4 slice. The times are simulated.
32 devices in a mesh: grp: 2 (over y), slab: 4 (over z), head: 2 (over x), seq: 2 (over core).
Axes of the slice: x: 2, y: 2, z: 4, core: 2. Of those that a mesh axis runs over, the one named last changes fastest.
Arguments:
- queries: bfloat16 [1024, 5120], P(('grp', 'seq'), 'head'), parts along dimension 0, may hold values from -140 to 140
- query_gain: float32 [5120], P('head'), may hold values from 1.5 to 3
- cache_keys: bfloat16 [4096, 5120], P(('grp', 'slab'), 'head'), parts along dimension 0, may hold values from -120 to 120
- cache_values: bfloat16 [4096, 5120], P(('grp', 'slab'), 'head'), parts along dimension 0, may hold values from -6 to 6
- finished_keys: bfloat16 [1024, 5120], P(('grp', 'slab', 'seq'), 'head'), parts along dimension 0, may hold values from -6 to 6
- finished_values: bfloat16 [1024, 5120], P(('grp', 'slab', 'seq'), 'head'), parts along dimension 0, may hold values from -6 to 6
- new_keys: bfloat16 [1024, 5120], P(('grp', 'slab', 'seq'), 'head'), parts along dimension 0, may hold values from -6 to 6
- new_values: bfloat16 [1024, 5120], P(('grp', 'slab', 'seq'), 'head'), parts along dimension 0, may hold values from -6 to 6
- out_weight: bfloat16 [5120, 5120], P('head', 'slab'), may hold values from -0.25 to 0.25
- time_weight: float32 [256, 5120], P(None, ('slab', 'head')), may hold values from -0.375 to 0.375
- owner: int32 [2], P('grp'), parts along dimension 0, may hold values from 0 to 3
- step: int32 [2], P('grp'), parts along dimension 0, may hold values from 0 to 999
Outputs:
- branch: bfloat16 [1024, 5120], P(('grp', 'seq'), ('slab', 'head')), parts along dimension 0
There are 2 independent parts, one for each index of `grp`. A program takes and returns all parts, laid end to end along the dimension named above; an argument that names none is the same for every part. Nothing has to cross between parts.
All inputs are finite; a program needn't handle non-finite values.
Results may differ from a plain program's by a relative error of at most 0.012.
Values may be sent and summed in bfloat16 or wider, within the bound.
A program may use at most 64 MiB of HBM per device.

v0:
```python
import functools
import math

import jax
import jax.numpy as jnp
from jax import lax
from jax.experimental import pallas as pl
from jax.experimental.pallas import tpu as pltpu
from jax.sharding import PartitionSpec as P

HEADS = 40
HD = 128
EPSILON = 1e-06
LOW = -1e30
LAG = 5
MESH = pl.DeviceIdType.MESH
F32 = jnp.float32
BF16 = jnp.bfloat16


def kernel(
    dims,
    aligned,
    q_ref,
    gain_ref,
    ck_ref,
    cv_ref,
    fk_ref,
    fv_ref,
    nk_ref,
    nv_ref,
    w_ref,
    tw_ref,
    owner_ref,
    step_ref,
    out_ref,
    q,
    qg,
    gain,
    kc,
    vc,
    kf,
    vf,
    w,
    tw,
    squares,
    scale,
    own_o,
    own_s,
    pre_o,
    pre_s,
    suf_o,
    suf_s,
    right_o,
    right_s,
    left_o,
    left_s,
    att,
    acc,
    gate,
    xs,
    xr,
    load_sem,
    fresh_sem,
    fresh_send,
    fresh_recv,
    sq_send,
    sq_recv,
    right_send,
    right_recv,
    left_send,
    left_recv,
    x_send,
    x_recv,
):
    n, heads_n, seq_n = dims
    rows, width = q_ref.shape
    hcount = width // HD
    z = lax.axis_index("slab")
    hx = lax.axis_index("head")
    sq = lax.axis_index("seq")

    groups = rows // HD
    chunks = groups * hcount
    loads = [
        pltpu.make_async_copy(src, dst, load_sem.at[i])
        for i, (src, dst) in enumerate(
            [(q_ref, q), (gain_ref, gain), (ck_ref, kc), (cv_ref, vc), (w_ref, w), (tw_ref, tw)]
        )
    ]
    loads[0].start()
    loads[1].start()
    barrier = pltpu.get_barrier_semaphore()
    for d in range(1, seq_n):
        pl.semaphore_signal(
            barrier, inc=1, device_id={"seq": lax.rem(sq + d, seq_n)}, device_id_type=MESH
        )
    for d in range(1, heads_n):
        pl.semaphore_signal(
            barrier, inc=1, device_id={"head": lax.rem(hx + d, heads_n)}, device_id_type=MESH
        )

    @pl.when(z > 0)
    def _():
        pl.semaphore_signal(barrier, inc=1, device_id={"slab": z - 1}, device_id_type=MESH)

    @pl.when(z < n - 1)
    def _():
        pl.semaphore_signal(barrier, inc=1, device_id={"slab": z + 1}, device_id_type=MESH)

    def clear(o_ref, s_ref):
        o_ref[...] = jnp.zeros_like(o_ref)
        s_ref[:, 0:1, :] = jnp.full((chunks, 1, HD), LOW, F32)
        s_ref[:, 1:2, :] = jnp.zeros((chunks, 1, HD), F32)

    @pl.when(z == 0)
    def _():
        clear(pre_o, pre_s)

    @pl.when(z == n - 1)
    def _():
        clear(suf_o, suf_s)

    ends = (z == 0).astype(jnp.int32) + (z == n - 1).astype(jnp.int32)
    pl.semaphore_wait(barrier, seq_n - 1 + heads_n - 1 + 2 - ends)

    fresh_src = [(fk_ref, kf, 0), (nk_ref, kf, 1), (fv_ref, vf, 0), (nv_ref, vf, 1)]
    first = max(hcount // 5, 1) * HD
    cuts = [slice(0, first), slice(first, width)]
    fresh_remote = [[], []]
    for k, cols in enumerate(cuts):
        for d in range(1, seq_n):
            for i, (src, dst, part) in enumerate(fresh_src):
                c = pltpu.make_async_remote_copy(
                    src_ref=src.at[:, cols],
                    dst_ref=dst.at[sq, part, :, cols],
                    send_sem=fresh_send.at[d - 1, k, i],
                    recv_sem=fresh_recv.at[d - 1, k, i],
                    device_id={"seq": lax.rem(sq + d, seq_n)},
                    device_id_type=MESH,
                )
                c.start()
                fresh_remote[k].append(c)

    loads[0].wait()
    loads[1].wait()
    loads[5].start()
    loads[2].start()
    loads[3].start()
    fresh_local = []
    for i, (src, dst, part) in enumerate(fresh_src):
        c = pltpu.make_async_copy(src, dst.at[sq, part], fresh_sem.at[i])
        c.start()
        fresh_local.append(c)
    loads[4].start()

    def squares_step(h, total):
        cols = pl.ds(pl.multiple_of(h * HD, HD), HD)
        x = q[:, cols].astype(F32)
        qg[:, cols] = (x * gain[cols][None, :]).astype(BF16)
        return total + x * x

    total = lax.fori_loop(0, hcount, squares_step, jnp.zeros((rows, HD), F32))
    row_total = jnp.sum(total.T, axis=0, keepdims=True)
    squares[hx] = jnp.broadcast_to(row_total, (8, rows))
    loads[5].wait()
    sq_copies = []
    for d in range(1, heads_n):
        c = pltpu.make_async_remote_copy(
            src_ref=squares.at[hx],
            dst_ref=squares.at[hx],
            send_sem=sq_send.at[d - 1],
            recv_sem=sq_recv.at[d - 1],
            device_id={"head": lax.rem(hx + d, heads_n)},
            device_id_type=MESH,
        )
        c.start()
        sq_copies.append(c)
    if aligned:
        half = tw.shape[0] // 2
        j = lax.broadcasted_iota(jnp.int32, (half, HD), 0).astype(F32)
        frequency = jnp.exp(F32(-math.log(10000.0)) * j / half)
        phases = jnp.full((half, HD), step_ref[0], jnp.int32).astype(F32) * frequency
        cos, sin = jnp.cos(phases), jnp.sin(phases)
        for c in range(tw.shape[1] // HD):
            cols = slice(c * HD, (c + 1) * HD)
            terms = tw[:half, cols] * cos + tw[half:, cols] * sin
            gate[:, cols] = 1.0 + jnp.sum(terms, axis=0, keepdims=True)

    for c in fresh_local + loads[2:4]:
        c.wait()
    for c in fresh_remote[0]:
        c.wait_recv()
    for c in sq_copies:
        c.wait_recv()
    norm_total = jnp.sum(squares[...], axis=0)
    scale[...] = lax.rsqrt(norm_total / (HEADS * HD) + EPSILON) * (
        math.log2(math.e) / HD**0.5
    )
    def send(h, direction):
        if direction > 0:
            pairs, ss, rs = ((right_o, pre_o), (right_s, pre_s)), right_send, right_recv
        else:
            pairs, ss, rs = ((left_o, suf_o), (left_s, suf_s)), left_send, left_recv
        return [
            pltpu.make_async_remote_copy(
                src_ref=src.at[h],
                dst_ref=dst.at[h],
                send_sem=ss.at[h, i],
                recv_sem=rs.at[h, i],
                device_id={"slab": z + direction},
                device_id_type=MESH,
            )
            for i, (src, dst) in enumerate(pairs)
        ]

    pair = 2 if hcount % 2 == 0 else 1
    fresh_rows = seq_n * 2 * fk_ref.shape[0]
    lag_end = LAG * jnp.maximum(z, n - 1 - z)

    def combine(h, other_o, other_s, dest_o, dest_s):
        m_a, l_a = own_s[h, 0:1], own_s[h, 1:2]
        m_b, l_b = other_s[h, 0:1], other_s[h, 1:2]
        top = jnp.maximum(m_a, m_b)
        e_a, e_b = jnp.exp2(m_a - top), jnp.exp2(m_b - top)
        dest_o[h] = (own_o[h] * e_a + other_o[h].astype(F32) * e_b).astype(BF16)
        dest_s[h, 0:1] = top
        dest_s[h, 1:2] = l_a * e_a + l_b * e_b

    nt = (((1,), (1,)), ((), ()))
    tn = (((0,), (0,)), ((), ()))

    def attend(h):
        cols = pl.ds(pl.multiple_of(h * HD, HD), HD)
        penalty = jnp.where(
            jnp.full((1, rows), owner_ref[0], jnp.int32) == z, F32(LOW), F32(0.0)
        )
        q_head = qg[:, cols]
        s_row = scale[0:1]
        s_c = (
            lax.dot_general(kc[:, cols], q_head, nt, preferred_element_type=F32) * s_row
            + penalty
        )
        k_fresh = kf[:, :, :, cols].reshape(fresh_rows, HD)
        v_fresh = vf[:, :, :, cols].reshape(fresh_rows, HD)
        s_f = lax.dot_general(k_fresh, q_head, nt, preferred_element_type=F32) * s_row
        top = jnp.maximum(
            jnp.max(s_c, axis=0, keepdims=True), jnp.max(s_f, axis=0, keepdims=True)
        )
        p_c = jnp.exp2(s_c - top)
        p_f = jnp.exp2(s_f - top)
        mass = jnp.sum(p_c, axis=0, keepdims=True) + jnp.sum(p_f, axis=0, keepdims=True)
        o = lax.dot_general(
            vc[:, cols], p_c.astype(BF16), tn, preferred_element_type=F32
        ) + lax.dot_general(v_fresh, p_f.astype(BF16), tn, preferred_element_type=F32)
        for g in range(groups):
            part = slice(g * HD, (g + 1) * HD)
            own_s[g * hcount + h, 0:1] = top[:, part]
            own_s[g * hcount + h, 1:2] = mass[:, part]
            own_o[g * hcount + h] = o[:, part]

    def project(g, p):
        deep = pl.ds(pl.multiple_of(p * pair * HD, HD), pair * HD)
        term = lax.dot_general(att[g, deep, :], w[deep, :], tn, preferred_element_type=F32)

        @pl.when(p == 0)
        def _():
            acc[g] = term

        @pl.when(p > 0)
        def _():
            acc[g] += term

    def exchange(g):
        copies = []
        for d in range(1, heads_n):
            copies.append(
                pltpu.make_async_remote_copy(
                    src_ref=xs.at[d - 1, g],
                    dst_ref=xr.at[d - 1, g],
                    send_sem=x_send.at[d - 1, g],
                    recv_sem=x_recv.at[d - 1, g],
                    device_id={"head": lax.rem(hx + d, heads_n)},
                    device_id_type=MESH,
                )
            )
        return copies

    def exchange_start(g):
        cp = out_ref.shape[1]
        for d, c in enumerate(exchange(g)):
            peer = lax.rem(hx + d + 1, heads_n)
            cols = pl.ds(pl.multiple_of(peer * cp, HD), cp)
            xs[d, g] = acc[g, :, cols].astype(BF16)
            c.start()

    pairs = hcount // pair
    last = (groups - 1) * hcount
    attend(0)

    def body(t, carry):
        cp_ = t - LAG * z
        in_p = (cp_ >= 0) & (cp_ < chunks)
        cs = t - LAG * (n - 1 - z)
        in_s = (cs >= 0) & (cs < chunks)

        @pl.when(in_p & (z > 0))
        def _():
            for c in send(cp_, 1):
                c.wait_recv()

        @pl.when(in_p & (z < n - 1))
        def _():
            combine(cp_, pre_o, pre_s, right_o, right_s)

        @pl.when(in_s & (z < n - 1))
        def _():
            for c in send(cs, -1):
                c.wait_recv()

        @pl.when(in_s & (z > 0))
        def _():
            combine(cs, suf_o, suf_s, left_o, left_s)

        f = t - lag_end

        @pl.when((f >= 0) & (f < chunks))
        def _():
            m_a, m_b, m_c = own_s[f, 0:1], pre_s[f, 0:1], suf_s[f, 0:1]
            top = jnp.maximum(m_a, jnp.maximum(m_b, m_c))
            e_a, e_b, e_c = jnp.exp2(m_a - top), jnp.exp2(m_b - top), jnp.exp2(m_c - top)
            mass = own_s[f, 1:2] * e_a + pre_s[f, 1:2] * e_b + suf_s[f, 1:2] * e_c
            total_o = (
                own_o[f] * e_a + pre_o[f].astype(F32) * e_b + suf_o[f].astype(F32) * e_c
            )
            h = lax.rem(f, hcount)
            att[f // hcount, pl.ds(pl.multiple_of(h * HD, HD), HD), :] = (
                total_o / mass
            ).astype(BF16)

        @pl.when(in_p & (z < n - 1))
        def _():
            for c in send(cp_, 1):
                c.start()

        @pl.when(in_s & (z > 0))
        def _():
            for c in send(cs, -1):
                c.start()

        @pl.when(t + 1 == first // HD)
        def _():
            for c in fresh_remote[1]:
                c.wait_recv()

        @pl.when(t + 1 < hcount)
        def _():
            attend(t + 1)

        @pl.when(f == last)
        def _():
            loads[4].wait()

        for g in range(groups - 1):

            @pl.when((f >= last) & (f < last + pairs))
            def _(g=g):
                project(g, f - last)

            if aligned:

                @pl.when(f == last + pairs - 1)
                def _(g=g):
                    exchange_start(g)

        done = f - last + 1

        @pl.when((done > 0) & (done <= hcount) & (lax.rem(done, pair) == 0))
        def _():
            project(groups - 1, done // pair - 1)

        return carry

    lax.fori_loop(0, chunks + LAG * (n - 1), body, 0)

    if aligned:
        cp = out_ref.shape[1]
        mine = pl.ds(pl.multiple_of(hx * cp, HD), cp)
        exchange_start(groups - 1)
        for g in range(groups):
            summed = acc[g, :, mine]
            for d, c in enumerate(exchange(g)):
                c.wait_recv()
                summed = summed + xr[d, g].astype(F32)
            out_ref[g * HD : (g + 1) * HD, :] = (summed * gate[...]).astype(out_ref.dtype)
        for g in range(groups):
            for c in exchange(g):
                c.wait_send()
    else:
        for g in range(groups):
            out_ref[g * HD : (g + 1) * HD, :] = acc[g]

    for c in fresh_remote[0] + fresh_remote[1] + sq_copies:
        c.wait_send()

    def drain(h, carry):
        @pl.when(z < n - 1)
        def _():
            for c in send(h, 1):
                c.wait_send()

        @pl.when(z > 0)
        def _():
            for c in send(h, -1):
                c.wait_send()

        return carry

    lax.fori_loop(0, chunks, drain, 0)


def local(sizes, *args):
    (
        queries,
        query_gain,
        cache_keys,
        cache_values,
        finished_keys,
        finished_values,
        new_keys,
        new_values,
        out_weight,
        time_weight,
        owner,
        step,
    ) = args
    n, heads_n, seq_n = sizes
    rows, width = queries.shape
    hcount = width // HD
    cached, fresh = cache_keys.shape[0], finished_keys.shape[0]
    columns, cp = out_weight.shape[1], time_weight.shape[1]
    freq = time_weight.shape[0]
    aligned = cp % HD == 0
    any_spec = pl.BlockSpec(memory_space=pl.ANY)
    smem = pl.BlockSpec(memory_space=pltpu.SMEM)
    vmem = pl.BlockSpec(memory_space=pltpu.VMEM)
    dma = pltpu.SemaphoreType.DMA
    xcount = max(heads_n - 1, 1)
    groups = rows // HD
    chunks = groups * hcount
    stat = (chunks, 2, HD)
    part = (chunks, HD, HD)
    result = pl.pallas_call(
        functools.partial(kernel, sizes, aligned),
        out_shape=jax.ShapeDtypeStruct(
            (rows, cp if aligned else columns), BF16 if aligned else F32
        ),
        in_specs=[any_spec] * 10 + [smem] * 2,
        out_specs=vmem,
        scratch_shapes=[
            pltpu.VMEM((rows, width), BF16),
            pltpu.VMEM((rows, width), BF16),
            pltpu.VMEM((width,), F32),
            pltpu.VMEM((cached, width), BF16),
            pltpu.VMEM((cached, width), BF16),
            pltpu.VMEM((seq_n, 2, fresh, width), BF16),
            pltpu.VMEM((seq_n, 2, fresh, width), BF16),
            pltpu.VMEM((width, columns), BF16),
            pltpu.VMEM((freq, cp), F32),
            pltpu.VMEM((heads_n, 8, rows), F32),
            pltpu.VMEM((8, rows), F32),
            pltpu.VMEM(part, F32),
            pltpu.VMEM(stat, F32),
            pltpu.VMEM(part, BF16),
            pltpu.VMEM(stat, F32),
            pltpu.VMEM(part, BF16),
            pltpu.VMEM(stat, F32),
            pltpu.VMEM(part, BF16),
            pltpu.VMEM(stat, F32),
            pltpu.VMEM(part, BF16),
            pltpu.VMEM(stat, F32),
            pltpu.VMEM((groups, width, HD), BF16),
            pltpu.VMEM((groups, HD, columns), F32),
            pltpu.VMEM((1, cp), F32),
            pltpu.VMEM((xcount, groups, HD, cp), BF16),
            pltpu.VMEM((xcount, groups, HD, cp), BF16),
            dma((6,)),
            dma((4,)),
            dma((max(seq_n - 1, 1), 2, 4)),
            dma((max(seq_n - 1, 1), 2, 4)),
            dma((xcount,)),
            dma((xcount,)),
            dma((chunks, 2)),
            dma((chunks, 2)),
            dma((chunks, 2)),
            dma((chunks, 2)),
            dma((xcount, groups)),
            dma((xcount, groups)),
        ],
        compiler_params=pltpu.CompilerParams(
            collective_id=0, has_side_effects=True, vmem_limit_bytes=60 * 1024 * 1024
        ),
        name="sweep_attention",
    )(
        queries,
        query_gain,
        cache_keys,
        cache_values,
        finished_keys,
        finished_values,
        new_keys,
        new_values,
        out_weight,
        time_weight,
        owner,
        step,
    )
    if aligned:
        return result
    summed = lax.psum_scatter(result, "head", scatter_dimension=1, tiled=True)
    half = freq // 2
    frequency = jnp.exp(-jnp.log(10000.0) * jnp.arange(half, dtype=F32) / half)
    phases = step[0].astype(F32) * frequency
    embedding = jnp.concatenate([jnp.cos(phases), jnp.sin(phases)])
    time_gate = 1.0 + jnp.dot(embedding, time_weight, precision=lax.Precision.HIGHEST)
    return (time_gate * summed).astype(BF16)


def solution(mesh):
    in_specs = (
        P(("grp", "seq"), "head"),
        P("head"),
        P(("grp", "slab"), "head"),
        P(("grp", "slab"), "head"),
        P(("grp", "slab", "seq"), "head"),
        P(("grp", "slab", "seq"), "head"),
        P(("grp", "slab", "seq"), "head"),
        P(("grp", "slab", "seq"), "head"),
        P("head", "slab"),
        P(None, ("slab", "head")),
        P("grp"),
        P("grp"),
    )
    out_specs = P(("grp", "seq"), ("slab", "head"))
    sizes = (mesh.shape["slab"], mesh.shape["head"], mesh.shape["seq"])
    return jax.shard_map(
        functools.partial(local, sizes),
        mesh=mesh,
        in_specs=in_specs,
        out_specs=out_specs,
        check_vma=False,
    )
```

profile of v0, /device:TPU:0, one launch (start us, length us, event | category | flops | bytes accessed | tf_op | source)
XLA Modules:
  0.0 60.3 jit_solution(14135727846626804923)
XLA Ops:
  1.3 57.3 %sweep_attention.1 = bf16[256,640]{1,0:T(8,128)(2,1)} custom-call(bf16[256,2560]{1,0:T(8,128)(2,1)} %q_ref.1, f32[2560]{0:T(1024)} %gain_ref.1, bf16[512,2560]{1,0:T(8,128)(2,1)} %ck_ref.1, bf16[512,2560]{1,0:T(8,128)(2,1)} %cv_ref.1, bf16[64,2560]{1,0:T(8,128)(2,1)} %fk_ref.1, bf16[64,2560]{1,0:T(8,128)(2,1)} %fv_ref.1, bf16[64,2560]{1,0:T(8,128)(2,1)} %nk_ref.1, ...), custom_call_target="tpu_custom_call" | custom-call | tf_op jit(solution)/shard_map/sweep_attention/pallas_call | solution.py:453
  58.6 1.7 %copy.16 = bf16[256,640]{1,0:T(8,128)(2,1)} copy(bf16[256,640]{1,0:T(8,128)(2,1)} %sweep_attention.1) | data formatting | bytes 655360
where the time goes:
time: 60.5 us; the launch traced here: 60.3 us
  Pallas kernels  57.3 us (95%)
  local copies, waits for them, and re-layouts  1.73 us (3%)
  between operations  1.3 us (2%)
    pallas_call x1, Pallas kernels, local(): pl.pallas_call(functools.partial(kernel, sizes, aligned), out_shape=jax.S...  57.3 us
    unnamed x1, local copies, waits for them, and re-layouts  1.73 us

commit v1 on v0

--- a/solution.py
+++ b/solution.py
@@ -72,6 +72,9 @@
     left_recv,
     x_send,
     x_recv,
+    s_buf,
+    p_buf,
+    m_buf,
 ):
     n, heads_n, seq_n = dims
     rows, width = q_ref.shape
@@ -125,9 +128,10 @@
     pl.semaphore_wait(barrier, seq_n - 1 + heads_n - 1 + 2 - ends)
 
     fresh_src = [(fk_ref, kf, 0), (nk_ref, kf, 1), (fv_ref, vf, 0), (nv_ref, vf, 1)]
-    first = max(hcount // 5, 1) * HD
-    cuts = [slice(0, first), slice(first, width)]
-    fresh_remote = [[], []]
+    ahead = min(max(hcount // 5, 3), hcount)
+    edges = [0, ahead * HD, width] if ahead < hcount else [0, width]
+    cuts = [slice(a, b) for a, b in zip(edges, edges[1:])]
+    fresh_remote = [[] for _ in cuts]
     for k, cols in enumerate(cuts):
         for d in range(1, seq_n):
             for i, (src, dst, part) in enumerate(fresh_src):
@@ -155,15 +159,12 @@
     loads[4].start()
 
     def squares_step(h, total):
-        cols = pl.ds(pl.multiple_of(h * HD, HD), HD)
-        x = q[:, cols].astype(F32)
-        qg[:, cols] = (x * gain[cols][None, :]).astype(BF16)
+        x = q[:, pl.ds(pl.multiple_of(h * HD, HD), HD)].astype(F32)
         return total + x * x
 
     total = lax.fori_loop(0, hcount, squares_step, jnp.zeros((rows, HD), F32))
     row_total = jnp.sum(total.T, axis=0, keepdims=True)
     squares[hx] = jnp.broadcast_to(row_total, (8, rows))
-    loads[5].wait()
     sq_copies = []
     for d in range(1, heads_n):
         c = pltpu.make_async_remote_copy(
@@ -176,6 +177,14 @@
         )
         c.start()
         sq_copies.append(c)
+
+    def gain_step(h, carry):
+        cols = pl.ds(pl.multiple_of(h * HD, HD), HD)
+        qg[:, cols] = (q[:, cols].astype(F32) * gain[cols][None, :]).astype(BF16)
+        return carry
+
+    lax.fori_loop(0, hcount, gain_step, 0)
+    loads[5].wait()
     if aligned:
         half = tw.shape[0] // 2
         j = lax.broadcasted_iota(jnp.int32, (half, HD), 0).astype(F32)
@@ -187,16 +196,7 @@
             terms = tw[:half, cols] * cos + tw[half:, cols] * sin
             gate[:, cols] = 1.0 + jnp.sum(terms, axis=0, keepdims=True)
 
-    for c in fresh_local + loads[2:4]:
-        c.wait()
-    for c in fresh_remote[0]:
-        c.wait_recv()
-    for c in sq_copies:
-        c.wait_recv()
-    norm_total = jnp.sum(squares[...], axis=0)
-    scale[...] = lax.rsqrt(norm_total / (HEADS * HD) + EPSILON) * (
-        math.log2(math.e) / HD**0.5
-    )
+
     def send(h, direction):
         if direction > 0:
             pairs, ss, rs = ((right_o, pre_o), (right_s, pre_s)), right_send, right_recv
@@ -230,34 +230,55 @@
     nt = (((1,), (1,)), ((), ()))
     tn = (((0,), (0,)), ((), ()))
 
-    def attend(h):
-        cols = pl.ds(pl.multiple_of(h * HD, HD), HD)
-        penalty = jnp.where(
-            jnp.full((1, rows), owner_ref[0], jnp.int32) == z, F32(LOW), F32(0.0)
-        )
+    penalty = jnp.where(
+        jnp.full((1, rows), owner_ref[0], jnp.int32) == z, F32(LOW), F32(0.0)
+    )
+    cached = kc.shape[0]
+    step_keys = 256 if cached % 256 == 0 else cached
+    blocks = [(i, i + step_keys) for i in range(0, cached, step_keys)]
+
+    def head_cols(h):
+        return pl.ds(pl.multiple_of(h * HD, HD), HD)
+
+    def scores(h, slot):
+        cols = head_cols(h)
         q_head = qg[:, cols]
+        top = None
+        for a, b in blocks:
+            part = lax.dot_general(kc[a:b, cols], q_head, nt, preferred_element_type=F32)
+            s_buf[slot, a:b, :] = part
+            high = jnp.max(part, axis=0, keepdims=True)
+            top = high if top is None else jnp.maximum(top, high)
+        k_fresh = kf[:, :, :, cols].reshape(fresh_rows, HD)
+        part = lax.dot_general(k_fresh, q_head, nt, preferred_element_type=F32)
+        s_buf[slot, cached:, :] = part
+        m_buf[slot, 0:1, :] = top
+        m_buf[slot, 1:2, :] = jnp.max(part, axis=0, keepdims=True)
+
+    def soften(h, slot):
         s_row = scale[0:1]
-        s_c = (
-            lax.dot_general(kc[:, cols], q_head, nt, preferred_element_type=F32) * s_row
-            + penalty
-        )
-        k_fresh = kf[:, :, :, cols].reshape(fresh_rows, HD)
-        v_fresh = vf[:, :, :, cols].reshape(fresh_rows, HD)
-        s_f = lax.dot_general(k_fresh, q_head, nt, preferred_element_type=F32) * s_row
-        top = jnp.maximum(
-            jnp.max(s_c, axis=0, keepdims=True), jnp.max(s_f, axis=0, keepdims=True)
-        )
-        p_c = jnp.exp2(s_c - top)
-        p_f = jnp.exp2(s_f - top)
-        mass = jnp.sum(p_c, axis=0, keepdims=True) + jnp.sum(p_f, axis=0, keepdims=True)
-        o = lax.dot_general(
-            vc[:, cols], p_c.astype(BF16), tn, preferred_element_type=F32
-        ) + lax.dot_general(v_fresh, p_f.astype(BF16), tn, preferred_element_type=F32)
+        top = jnp.maximum(m_buf[slot, 0:1, :] * s_row + penalty, m_buf[slot, 1:2, :] * s_row)
+        top_c = top - penalty
+        mass = jnp.zeros((1, rows), F32)
+        for a, b in blocks + [(cached, cached + fresh_rows)]:
+            p = jnp.exp2(s_buf[slot, a:b, :] * s_row - (top_c if a < cached else top))
+            p_buf[slot, a:b, :] = p.astype(BF16)
+            mass = mass + jnp.sum(p, axis=0, keepdims=True)
         for g in range(groups):
             part = slice(g * HD, (g + 1) * HD)
             own_s[g * hcount + h, 0:1] = top[:, part]
             own_s[g * hcount + h, 1:2] = mass[:, part]
-            own_o[g * hcount + h] = o[:, part]
+
+    def weigh(h, slot):
+        cols = head_cols(h)
+        v_fresh = vf[:, :, :, cols].reshape(fresh_rows, HD)
+        o = lax.dot_general(v_fresh, p_buf[slot, cached:, :], tn, preferred_element_type=F32)
+        for a, b in blocks:
+            o += lax.dot_general(
+                vc[a:b, cols], p_buf[slot, a:b, :], tn, preferred_element_type=F32
+            )
+        for g in range(groups):
+            own_o[g * hcount + h] = o[:, g * HD : (g + 1) * HD]
 
     def project(g, p):
         deep = pl.ds(pl.multiple_of(p * pair * HD, HD), pair * HD)
@@ -296,9 +317,8 @@
 
     pairs = hcount // pair
     last = (groups - 1) * hcount
-    attend(0)
-
-    def body(t, carry):
+
+    def service(t):
         cp_ = t - LAG * z
         in_p = (cp_ >= 0) & (cp_ < chunks)
         cs = t - LAG * (n - 1 - z)
@@ -312,6 +332,8 @@
         @pl.when(in_p & (z < n - 1))
         def _():
             combine(cp_, pre_o, pre_s, right_o, right_s)
+            for c in send(cp_, 1):
+                c.start()
 
         @pl.when(in_s & (z < n - 1))
         def _():
@@ -321,7 +343,10 @@
         @pl.when(in_s & (z > 0))
         def _():
             combine(cs, suf_o, suf_s, left_o, left_s)
-
+            for c in send(cs, -1):
+                c.start()
+
+    def finish(t):
         f = t - lag_end
 
         @pl.when((f >= 0) & (f < chunks))
@@ -338,25 +363,6 @@
                 total_o / mass
             ).astype(BF16)
 
-        @pl.when(in_p & (z < n - 1))
-        def _():
-            for c in send(cp_, 1):
-                c.start()
-
-        @pl.when(in_s & (z > 0))
-        def _():
-            for c in send(cs, -1):
-                c.start()
-
-        @pl.when(t + 1 == first // HD)
-        def _():
-            for c in fresh_remote[1]:
-                c.wait_recv()
-
-        @pl.when(t + 1 < hcount)
-        def _():
-            attend(t + 1)
-
         @pl.when(f == last)
         def _():
             loads[4].wait()
@@ -379,14 +385,74 @@
         def _():
             project(groups - 1, done // pair - 1)
 
+    def near(h):
+        return jnp.minimum(h, hcount - 1)
+
+    loads[2].wait()
+    for c in fresh_local:
+        c.wait()
+    for c in fresh_remote[0]:
+        c.wait_recv()
+    scores(0, 0)
+    scores(min(1, hcount - 1), 1)
+    for c in sq_copies:
+        c.wait_recv()
+    norm_total = jnp.sum(squares[...], axis=0)
+    scale[...] = lax.rsqrt(norm_total / (HEADS * HD) + EPSILON) * (
+        math.log2(math.e) / HD**0.5
+    )
+    soften(0, 0)
+    loads[3].wait()
+    weigh(0, 0)
+    service(0)
+    soften(min(1, hcount - 1), 1)
+    scores(min(2, hcount - 1), 0)
+
+    def body(i, carry):
+        for u in range(2):
+            t = 2 * i + u
+            if len(cuts) > 1:
+
+                @pl.when(t + 3 == ahead)
+                def _():
+                    for c in fresh_remote[1]:
+                        c.wait_recv()
+
+            @pl.when(t + 1 < hcount)
+            def _(t=t, u=u):
+                scores(near(t + 3), 1 - u)
+                soften(near(t + 2), u)
+                weigh(near(t + 1), 1 - u)
+
+            finish(t)
+            service(t + 1)
         return carry
 
-    lax.fori_loop(0, chunks + LAG * (n - 1), body, 0)
+    lax.fori_loop(0, (chunks + LAG * (n - 1) + 1) // 2, body, 0)
+
+    def drain(h, carry):
+        @pl.when(z < n - 1)
+        def _():
+            for c in send(h, 1):
+                c.wait_send()
+
+        @pl.when(z > 0)
+        def _():
+            for c in send(h, -1):
+                c.wait_send()
+
+        return carry
+
+    def settle():
+        for c in [c for cut in fresh_remote for c in cut] + sq_copies:
+            c.wait_send()
+        lax.fori_loop(0, chunks, drain, 0)
 
     if aligned:
         cp = out_ref.shape[1]
         mine = pl.ds(pl.multiple_of(hx * cp, HD), cp)
         exchange_start(groups - 1)
+        settle()
         for g in range(groups):
             summed = acc[g, :, mine]
             for d, c in enumerate(exchange(g)):
@@ -399,24 +465,7 @@
     else:
         for g in range(groups):
             out_ref[g * HD : (g + 1) * HD, :] = acc[g]
-
-    for c in fresh_remote[0] + fresh_remote[1] + sq_copies:
-        c.wait_send()
-
-    def drain(h, carry):
-        @pl.when(z < n - 1)
-        def _():
-            for c in send(h, 1):
-                c.wait_send()
-
-        @pl.when(z > 0)
-        def _():
-            for c in send(h, -1):
-                c.wait_send()
-
-        return carry
-
-    lax.fori_loop(0, chunks, drain, 0)
+        settle()
 
 
 def local(sizes, *args):
@@ -449,6 +498,7 @@
     groups = rows // HD
     chunks = groups * hcount
     stat = (chunks, 2, HD)
+    keys = cached + seq_n * 2 * fresh
     part = (chunks, HD, HD)
     result = pl.pallas_call(
         functools.partial(kernel, sizes, aligned),
@@ -496,6 +546,9 @@
             dma((chunks, 2)),
             dma((xcount, groups)),
             dma((xcount, groups)),
+            pltpu.VMEM((2, keys, rows), F32),
+            pltpu.VMEM((2, keys, rows), BF16),
+            pltpu.VMEM((2, 2, rows), F32),
         ],
         compiler_params=pltpu.CompilerParams(
             collective_id=0, has_side_effects=True, vmem_limit_bytes=60 * 1024 * 1024

time: 60.5 us -> 57.5 us (0.950)
  Pallas kernels: 57.3 us -> 54.3 us
    pallas_call x1, Pallas kernels: 57.3 us -> 54.3 us  [local(): pl.pallas_call(functools.partial(kernel, sizes, aligned), out_shape=jax.S...]
where the time goes in v1:
time: 57.5 us; the launch traced here: 57.3 us
  Pallas kernels  54.3 us (94%)
  local copies, waits for them, and re-layouts  1.73 us (3%)
  between operations  1.3 us (2%)
    pallas_call x1, Pallas kernels, local(): pl.pallas_call(functools.partial(kernel, sizes, aligned), out_shape=jax.S...  54.3 us
    unnamed x1, local copies, waits for them, and re-layouts  1.73 us

profile of v1, /device:TPU:0, one launch (start us, length us, event | category | flops | bytes accessed | tf_op | source)
XLA Modules:
  0.0 57.3 jit_solution(2530574932241303973)
XLA Ops:
  1.3 54.3 %sweep_attention.1 = bf16[256,640]{1,0:T(8,128)(2,1)} custom-call(bf16[256,2560]{1,0:T(8,128)(2,1)} %q_ref.1, f32[2560]{0:T(1024)} %gain_ref.1, bf16[512,2560]{1,0:T(8,128)(2,1)} %ck_ref.1, bf16[512,2560]{1,0:T(8,128)(2,1)} %cv_ref.1, bf16[64,2560]{1,0:T(8,128)(2,1)} %fk_ref.1, bf16[64,2560]{1,0:T(8,128)(2,1)} %fv_ref.1, bf16[64,2560]{1,0:T(8,128)(2,1)} %nk_ref.1, ...), custom_call_target="tpu_custom_call" | custom-call | tf_op jit(solution)/shard_map/sweep_attention/pallas_call | solution.py:503
  55.6 1.7 %copy.16 = bf16[256,640]{1,0:T(8,128)(2,1)} copy(bf16[256,640]{1,0:T(8,128)(2,1)} %sweep_attention.1) | data formatting | bytes 655360

commit v2 on v1

--- a/solution.py
+++ b/solution.py
@@ -215,6 +215,10 @@
         ]
 
     pair = 2 if hcount % 2 == 0 else 1
+    splits = pair
+    sub = HD // splits
+    pairs = hcount // pair
+    last = (groups - 1) * hcount
     fresh_rows = seq_n * 2 * fk_ref.shape[0]
     lag_end = LAG * jnp.maximum(z, n - 1 - z)
 
@@ -264,10 +268,18 @@
             p = jnp.exp2(s_buf[slot, a:b, :] * s_row - (top_c if a < cached else top))
             p_buf[slot, a:b, :] = p.astype(BF16)
             mass = mass + jnp.sum(p, axis=0, keepdims=True)
-        for g in range(groups):
-            part = slice(g * HD, (g + 1) * HD)
-            own_s[g * hcount + h, 0:1] = top[:, part]
-            own_s[g * hcount + h, 1:2] = mass[:, part]
+        m_buf[slot, 2:3, :] = top
+        m_buf[slot, 3:4, :] = mass
+
+    def place(g, h, slot, value, store):
+        if g < groups - 1 or splits == 1:
+            store(g * hcount + h, slice(0, HD), value)
+            return
+        turned = pltpu.roll(value, sub, 1)
+        lanes = slice(slot * sub, (slot + 1) * sub)
+        for s in range(splits):
+            source = value if s == slot else turned
+            store(last + s * pairs + lax.div(h, 2), lanes, source[:, lanes])
 
     def weigh(h, slot):
         cols = head_cols(h)
@@ -278,45 +290,65 @@
                 vc[a:b, cols], p_buf[slot, a:b, :], tn, preferred_element_type=F32
             )
         for g in range(groups):
-            own_o[g * hcount + h] = o[:, g * HD : (g + 1) * HD]
+            part = slice(g * HD, (g + 1) * HD)
+
+            def store_o(c, lanes, value):
+                own_o[c, :, lanes] = value
+
+            def store_s(c, lanes, value):
+                own_s[c, :, lanes] = value
+
+            place(g, h, slot, o[:, part], store_o)
+            place(g, h, slot, m_buf[slot, 2:4, part], store_s)
 
     def project(g, p):
         deep = pl.ds(pl.multiple_of(p * pair * HD, HD), pair * HD)
         term = lax.dot_general(att[g, deep, :], w[deep, :], tn, preferred_element_type=F32)
-
+        add(acc.at[g * HD : (g + 1) * HD, :], term, p)
+
+    def project_last(s, p):
+        deep = pl.ds(pl.multiple_of(p * pair * HD, HD), pair * HD)
+        term = lax.dot_general(
+            att[groups - 1 + s, deep, 0:sub], w[deep, :], tn, preferred_element_type=F32
+        )
+        add(acc.at[(groups - 1) * HD + s * sub : (groups - 1) * HD + (s + 1) * sub, :], term, p)
+
+    def add(dest, term, p):
         @pl.when(p == 0)
         def _():
-            acc[g] = term
+            dest[...] = term
 
         @pl.when(p > 0)
         def _():
-            acc[g] += term
-
-    def exchange(g):
+            dest[...] += term
+
+    pieces = [(g * HD, (g + 1) * HD) for g in range(groups - 1)]
+    pieces += [((groups - 1) * HD + s * sub, (groups - 1) * HD + (s + 1) * sub) for s in range(splits)]
+
+    def exchange(k):
+        a, b = pieces[k]
         copies = []
         for d in range(1, heads_n):
             copies.append(
                 pltpu.make_async_remote_copy(
-                    src_ref=xs.at[d - 1, g],
-                    dst_ref=xr.at[d - 1, g],
-                    send_sem=x_send.at[d - 1, g],
-                    recv_sem=x_recv.at[d - 1, g],
+                    src_ref=xs.at[d - 1, a:b],
+                    dst_ref=xr.at[d - 1, a:b],
+                    send_sem=x_send.at[d - 1, k],
+                    recv_sem=x_recv.at[d - 1, k],
                     device_id={"head": lax.rem(hx + d, heads_n)},
                     device_id_type=MESH,
                 )
             )
         return copies
 
-    def exchange_start(g):
+    def exchange_start(k):
+        a, b = pieces[k]
         cp = out_ref.shape[1]
-        for d, c in enumerate(exchange(g)):
+        for d, c in enumerate(exchange(k)):
             peer = lax.rem(hx + d + 1, heads_n)
             cols = pl.ds(pl.multiple_of(peer * cp, HD), cp)
-            xs[d, g] = acc[g, :, cols].astype(BF16)
+            xs[d, a:b] = acc[a:b, cols].astype(BF16)
             c.start()
-
-    pairs = hcount // pair
-    last = (groups - 1) * hcount
 
     def service(t):
         cp_ = t - LAG * z
@@ -358,10 +390,20 @@
             total_o = (
                 own_o[f] * e_a + pre_o[f].astype(F32) * e_b + suf_o[f].astype(F32) * e_c
             )
-            h = lax.rem(f, hcount)
-            att[f // hcount, pl.ds(pl.multiple_of(h * HD, HD), HD), :] = (
-                total_o / mass
-            ).astype(BF16)
+            value = (total_o / mass).astype(BF16)
+
+            @pl.when(f < last)
+            def _():
+                h = lax.rem(f, hcount)
+                att[f // hcount, head_cols(h), :] = value
+
+            @pl.when(f >= last)
+            def _():
+                k = f - last
+                s, p = lax.div(k, pairs), lax.rem(k, pairs)
+                for i in range(pair):
+                    turned = value if i == 0 else pltpu.roll(total_o / mass, HD - i * sub, 1).astype(BF16)
+                    att[groups - 1 + s, head_cols(p * pair + i), :] = turned
 
         @pl.when(f == last)
         def _():
@@ -379,11 +421,18 @@
                 def _(g=g):
                     exchange_start(g)
 
-        done = f - last + 1
-
-        @pl.when((done > 0) & (done <= hcount) & (lax.rem(done, pair) == 0))
-        def _():
-            project(groups - 1, done // pair - 1)
+        for s in range(splits):
+            begin = last + s * pairs
+
+            @pl.when((f >= begin) & (f < begin + pairs))
+            def _(s=s, begin=begin):
+                project_last(s, f - begin)
+
+            if aligned and s < splits - 1:
+
+                @pl.when(f == begin + pairs - 1)
+                def _(s=s):
+                    exchange_start(groups - 1 + s)
 
     def near(h):
         return jnp.minimum(h, hcount - 1)
@@ -451,20 +500,19 @@
     if aligned:
         cp = out_ref.shape[1]
         mine = pl.ds(pl.multiple_of(hx * cp, HD), cp)
-        exchange_start(groups - 1)
+        exchange_start(len(pieces) - 1)
         settle()
-        for g in range(groups):
-            summed = acc[g, :, mine]
-            for d, c in enumerate(exchange(g)):
+        for k, (a, b) in enumerate(pieces):
+            summed = acc[a:b, mine]
+            for d, c in enumerate(exchange(k)):
                 c.wait_recv()
-                summed = summed + xr[d, g].astype(F32)
-            out_ref[g * HD : (g + 1) * HD, :] = (summed * gate[...]).astype(out_ref.dtype)
-        for g in range(groups):
-            for c in exchange(g):
+                summed = summed + xr[d, a:b].astype(F32)
+            out_ref[a:b, :] = (summed * gate[...]).astype(out_ref.dtype)
+        for k in range(len(pieces)):
+            for c in exchange(k):
                 c.wait_send()
     else:
-        for g in range(groups):
-            out_ref[g * HD : (g + 1) * HD, :] = acc[g]
+        out_ref[...] = acc[...]
         settle()
 
 
@@ -502,9 +550,7 @@
     part = (chunks, HD, HD)
     result = pl.pallas_call(
         functools.partial(kernel, sizes, aligned),
-        out_shape=jax.ShapeDtypeStruct(
-            (rows, cp if aligned else columns), BF16 if aligned else F32
-        ),
+        out_shape=pltpu.VMEM((rows, cp), BF16) if aligned else jax.ShapeDtypeStruct((rows, columns), F32),
         in_specs=[any_spec] * 10 + [smem] * 2,
         out_specs=vmem,
         scratch_shapes=[
@@ -529,11 +575,11 @@
             pltpu.VMEM(stat, F32),
             pltpu.VMEM(part, BF16),
             pltpu.VMEM(stat, F32),
-            pltpu.VMEM((groups, width, HD), BF16),
-            pltpu.VMEM((groups, HD, columns), F32),
+            pltpu.VMEM((groups + 1, width, HD), BF16),
+            pltpu.VMEM((rows, columns), F32),
             pltpu.VMEM((1, cp), F32),
-            pltpu.VMEM((xcount, groups, HD, cp), BF16),
-            pltpu.VMEM((xcount, groups, HD, cp), BF16),
+            pltpu.VMEM((xcount, rows, cp), BF16),
+            pltpu.VMEM((xcount, rows, cp), BF16),
             dma((6,)),
             dma((4,)),
             dma((max(seq_n - 1, 1), 2, 4)),
@@ -544,11 +590,11 @@
             dma((chunks, 2)),
             dma((chunks, 2)),
             dma((chunks, 2)),
-            dma((xcount, groups)),
-            dma((xcount, groups)),
+            dma((xcount, groups + 1)),
+            dma((xcount, groups + 1)),
             pltpu.VMEM((2, keys, rows), F32),
             pltpu.VMEM((2, keys, rows), BF16),
-            pltpu.VMEM((2, 2, rows), F32),
+            pltpu.VMEM((2, 4, rows), F32),
         ],
         compiler_params=pltpu.CompilerParams(
             collective_id=0, has_side_effects=True, vmem_limit_bytes=60 * 1024 * 1024

time: 57.5 us -> 56 us (0.974)
  local copies, waits for them, and re-layouts: 1.73 us -> 0.73 us
    unnamed x1, local copies, waits for them, and re-layouts: 1.73 us -> 0.73 us
where the time goes in v2:
time: 56 us; the launch traced here: 55.9 us
  Pallas kernels  53.8 us (96%)
  between operations  1.3 us (2%)
  local copies, waits for them, and re-layouts  0.73 us (1%)
    pallas_call x1, Pallas kernels, local(): pl.pallas_call(functools.partial(kernel, sizes, aligned), out_shape=pltpu...  53.8 us

profile of v2, /device:TPU:0, one launch (start us, length us, event | category | flops | bytes accessed | tf_op | source)
XLA Modules:
  0.0 55.9 jit_solution(483102693275032733)
XLA Ops:
  1.3 53.8 %sweep_attention.1 = bf16[256,640]{1,0:T(8,128)(2,1)S(1)} custom-call(bf16[256,2560]{1,0:T(8,128)(2,1)} %q_ref.1, f32[2560]{0:T(1024)} %gain_ref.1, bf16[512,2560]{1,0:T(8,128)(2,1)} %ck_ref.1, bf16[512,2560]{1,0:T(8,128)(2,1)} %cv_ref.1, bf16[64,2560]{1,0:T(8,128)(2,1)} %fk_ref.1, bf16[64,2560]{1,0:T(8,128)(2,1)} %fv_ref.1, bf16[64,2560]{1,0:T(8,128)(2,1)} %nk_ref.1, ...), custom_call_target="tpu_custom_call" | custom-call | tf_op jit(solution)/shard_map/sweep_attention/pallas_call | solution.py:551
  55.1 0.7 %copy.14 = bf16[256,640]{1,0:T(8,128)(2,1)} copy(bf16[256,640]{1,0:T(8,128)(2,1)S(1)} %sweep_attention.1) | data formatting | bytes 655360

commit v3 on v2

--- a/solution.py
+++ b/solution.py
@@ -13,6 +13,8 @@
 EPSILON = 1e-06
 LOW = -1e30
 LAG = 5
+SPLIT = 4
+PARTS = 4
 MESH = pl.DeviceIdType.MESH
 F32 = jnp.float32
 BF16 = jnp.bfloat16
@@ -75,6 +77,8 @@
     s_buf,
     p_buf,
     m_buf,
+    q_sem,
+    kv_sem,
 ):
     n, heads_n, seq_n = dims
     rows, width = q_ref.shape
@@ -91,7 +95,17 @@
             [(q_ref, q), (gain_ref, gain), (ck_ref, kc), (cv_ref, vc), (w_ref, w), (tw_ref, tw)]
         )
     ]
-    loads[0].start()
+    ahead = min(max(hcount // 5, 3), hcount)
+    parts = PARTS if hcount % PARTS == 0 else 1
+    span = width // parts
+    q_loads = [
+        pltpu.make_async_copy(
+            q_ref.at[:, k * span : (k + 1) * span], q.at[:, k * span : (k + 1) * span], q_sem.at[k]
+        )
+        for k in range(parts)
+    ]
+    for c in q_loads:
+        c.start()
     loads[1].start()
     barrier = pltpu.get_barrier_semaphore()
     for d in range(1, seq_n):
@@ -124,47 +138,35 @@
     def _():
         clear(suf_o, suf_s)
 
-    ends = (z == 0).astype(jnp.int32) + (z == n - 1).astype(jnp.int32)
-    pl.semaphore_wait(barrier, seq_n - 1 + heads_n - 1 + 2 - ends)
-
-    fresh_src = [(fk_ref, kf, 0), (nk_ref, kf, 1), (fv_ref, vf, 0), (nv_ref, vf, 1)]
-    ahead = min(max(hcount // 5, 3), hcount)
-    edges = [0, ahead * HD, width] if ahead < hcount else [0, width]
-    cuts = [slice(a, b) for a, b in zip(edges, edges[1:])]
-    fresh_remote = [[] for _ in cuts]
-    for k, cols in enumerate(cuts):
-        for d in range(1, seq_n):
-            for i, (src, dst, part) in enumerate(fresh_src):
-                c = pltpu.make_async_remote_copy(
-                    src_ref=src.at[:, cols],
-                    dst_ref=dst.at[sq, part, :, cols],
-                    send_sem=fresh_send.at[d - 1, k, i],
-                    recv_sem=fresh_recv.at[d - 1, k, i],
-                    device_id={"seq": lax.rem(sq + d, seq_n)},
-                    device_id_type=MESH,
-                )
-                c.start()
-                fresh_remote[k].append(c)
-
-    loads[0].wait()
-    loads[1].wait()
-    loads[5].start()
-    loads[2].start()
-    loads[3].start()
-    fresh_local = []
-    for i, (src, dst, part) in enumerate(fresh_src):
-        c = pltpu.make_async_copy(src, dst.at[sq, part], fresh_sem.at[i])
-        c.start()
-        fresh_local.append(c)
-    loads[4].start()
-
     def squares_step(h, total):
         x = q[:, pl.ds(pl.multiple_of(h * HD, HD), HD)].astype(F32)
         return total + x * x
 
-    total = lax.fori_loop(0, hcount, squares_step, jnp.zeros((rows, HD), F32))
+    total = jnp.zeros((rows, HD), F32)
+    for k, c in enumerate(q_loads):
+        c.wait()
+        total = lax.fori_loop(k * hcount // parts, (k + 1) * hcount // parts, squares_step, total)
+    head_cut = ahead * HD
+    kv_cuts = [slice(0, head_cut), slice(head_cut, width)] if head_cut < width else [slice(0, width)]
+    kv_loads = []
+    for k, cols in enumerate(kv_cuts):
+        for i, (src, dst) in enumerate([(ck_ref, kc), (cv_ref, vc)]):
+            kv_loads.append(pltpu.make_async_copy(src.at[:, cols], dst.at[:, cols], kv_sem.at[k, i]))
+    fresh_src = [(fk_ref, kf, 0), (nk_ref, kf, 1), (fv_ref, vf, 0), (nv_ref, vf, 1)]
+    loads[5].start()
+    for c in kv_loads:
+        c.start()
+    fresh_local = []
+    for i, (src, dst, part) in enumerate(fresh_src):
+        pltpu.make_async_copy(src, dst.at[sq, part], fresh_sem.at[i // 2]).start()
+    for side, whole in enumerate((kf, vf)):
+        fresh_local.append(pltpu.make_async_copy(whole.at[sq], whole.at[sq], fresh_sem.at[side]))
     row_total = jnp.sum(total.T, axis=0, keepdims=True)
     squares[hx] = jnp.broadcast_to(row_total, (8, rows))
+
+    ends = (z == 0).astype(jnp.int32) + (z == n - 1).astype(jnp.int32)
+    pl.semaphore_wait(barrier, seq_n - 1 + heads_n - 1 + 2 - ends)
+
     sq_copies = []
     for d in range(1, heads_n):
         c = pltpu.make_async_remote_copy(
@@ -178,6 +180,36 @@
         c.start()
         sq_copies.append(c)
 
+    edges = [0, ahead * HD, width] if ahead < hcount else [0, width]
+    cuts = [slice(a, b) for a, b in zip(edges, edges[1:])]
+    fresh_remote = [[] for _ in cuts]
+
+    def fresh_wait(d, side, cols, k=0):
+        whole = (kf, vf)[side].at[sq, :, :, cols]
+        return pltpu.make_async_remote_copy(
+            src_ref=whole,
+            dst_ref=whole,
+            send_sem=fresh_send.at[d - 1, side],
+            recv_sem=fresh_recv.at[d - 1, k, side],
+            device_id={"seq": lax.rem(sq + d, seq_n)},
+            device_id_type=MESH,
+        )
+
+    for k, cols in enumerate(cuts):
+        for d in range(1, seq_n):
+            for i, (src, dst, part) in enumerate(fresh_src):
+                pltpu.make_async_remote_copy(
+                    src_ref=src.at[:, cols],
+                    dst_ref=dst.at[sq, part, :, cols],
+                    send_sem=fresh_send.at[d - 1, i // 2],
+                    recv_sem=fresh_recv.at[d - 1, k, i // 2],
+                    device_id={"seq": lax.rem(sq + d, seq_n)},
+                    device_id_type=MESH,
+                ).start()
+            fresh_remote[k] += [fresh_wait(d, side, cols, k) for side in (0, 1)]
+
+    loads[1].wait()
+
     def gain_step(h, carry):
         cols = pl.ds(pl.multiple_of(h * HD, HD), HD)
         qg[:, cols] = (q[:, cols].astype(F32) * gain[cols][None, :]).astype(BF16)
@@ -197,6 +229,8 @@
             gate[:, cols] = 1.0 + jnp.sum(terms, axis=0, keepdims=True)
 
 
+    ring = min(chunks, LAG * (n - 1) + 1)
+
     def send(h, direction):
         if direction > 0:
             pairs, ss, rs = ((right_o, pre_o), (right_s, pre_s)), right_send, right_recv
@@ -206,17 +240,33 @@
             pltpu.make_async_remote_copy(
                 src_ref=src.at[h],
                 dst_ref=dst.at[h],
-                send_sem=ss.at[h, i],
-                recv_sem=rs.at[h, i],
+                send_sem=ss.at[i],
+                recv_sem=rs.at[lax.rem(h, ring), i],
                 device_id={"slab": z + direction},
                 device_id_type=MESH,
             )
             for i, (src, dst) in enumerate(pairs)
         ]
 
+    def settle_sends(direction):
+        if direction > 0:
+            pairs, ss, rs = ((right_o, pre_o), (right_s, pre_s)), right_send, right_recv
+        else:
+            pairs, ss, rs = ((left_o, suf_o), (left_s, suf_s)), left_send, left_recv
+        for i, (src, dst) in enumerate(pairs):
+            pltpu.make_async_remote_copy(
+                src_ref=src,
+                dst_ref=dst,
+                send_sem=ss.at[i],
+                recv_sem=rs.at[0, i],
+                device_id={"slab": z + direction},
+                device_id_type=MESH,
+            ).wait_send()
+
     pair = 2 if hcount % 2 == 0 else 1
-    splits = pair
+    splits = next(k for k in (SPLIT, 2, 1) if hcount % k == 0)
     sub = HD // splits
+    tuples = hcount // splits
     pairs = hcount // pair
     last = (groups - 1) * hcount
     fresh_rows = seq_n * 2 * fk_ref.shape[0]
@@ -271,17 +321,16 @@
         m_buf[slot, 2:3, :] = top
         m_buf[slot, 3:4, :] = mass
 
-    def place(g, h, slot, value, store):
+    def place(g, h, seat, value, store):
         if g < groups - 1 or splits == 1:
             store(g * hcount + h, slice(0, HD), value)
             return
-        turned = pltpu.roll(value, sub, 1)
-        lanes = slice(slot * sub, (slot + 1) * sub)
+        lanes = slice(seat * sub, (seat + 1) * sub)
         for s in range(splits):
-            source = value if s == slot else turned
-            store(last + s * pairs + lax.div(h, 2), lanes, source[:, lanes])
-
-    def weigh(h, slot):
+            source = value if s == seat else pltpu.roll(value, (seat - s) % splits * sub, 1)
+            store(last + s * tuples + lax.div(h, splits), lanes, source[:, lanes])
+
+    def weigh(h, slot, seat):
         cols = head_cols(h)
         v_fresh = vf[:, :, :, cols].reshape(fresh_rows, HD)
         o = lax.dot_general(v_fresh, p_buf[slot, cached:, :], tn, preferred_element_type=F32)
@@ -298,8 +347,8 @@
             def store_s(c, lanes, value):
                 own_s[c, :, lanes] = value
 
-            place(g, h, slot, o[:, part], store_o)
-            place(g, h, slot, m_buf[slot, 2:4, part], store_s)
+            place(g, h, seat, o[:, part], store_o)
+            place(g, h, seat, m_buf[slot, 2:4, part], store_s)
 
     def project(g, p):
         deep = pl.ds(pl.multiple_of(p * pair * HD, HD), pair * HD)
@@ -307,7 +356,7 @@
         add(acc.at[g * HD : (g + 1) * HD, :], term, p)
 
     def project_last(s, p):
-        deep = pl.ds(pl.multiple_of(p * pair * HD, HD), pair * HD)
+        deep = pl.ds(pl.multiple_of(p * splits * HD, HD), splits * HD)
         term = lax.dot_general(
             att[groups - 1 + s, deep, 0:sub], w[deep, :], tn, preferred_element_type=F32
         )
@@ -333,7 +382,7 @@
                 pltpu.make_async_remote_copy(
                     src_ref=xs.at[d - 1, a:b],
                     dst_ref=xr.at[d - 1, a:b],
-                    send_sem=x_send.at[d - 1, k],
+                    send_sem=x_send.at[d - 1],
                     recv_sem=x_recv.at[d - 1, k],
                     device_id={"head": lax.rem(hx + d, heads_n)},
                     device_id_type=MESH,
@@ -400,44 +449,45 @@
             @pl.when(f >= last)
             def _():
                 k = f - last
-                s, p = lax.div(k, pairs), lax.rem(k, pairs)
-                for i in range(pair):
+                s, p = lax.div(k, tuples), lax.rem(k, tuples)
+                for i in range(splits):
                     turned = value if i == 0 else pltpu.roll(total_o / mass, HD - i * sub, 1).astype(BF16)
-                    att[groups - 1 + s, head_cols(p * pair + i), :] = turned
-
-        @pl.when(f == last)
+                    att[groups - 1 + s, head_cols(p * splits + i), :] = turned
+
+        @pl.when(f == hcount - pairs)
         def _():
             loads[4].wait()
 
         for g in range(groups - 1):
-
-            @pl.when((f >= last) & (f < last + pairs))
-            def _(g=g):
-                project(g, f - last)
+            begin = (g + 1) * hcount - pairs
+
+            @pl.when((f >= begin) & (f < begin + pairs))
+            def _(g=g, begin=begin):
+                project(g, f - begin)
 
             if aligned:
 
-                @pl.when(f == last + pairs - 1)
+                @pl.when(f == begin + pairs - 1)
                 def _(g=g):
                     exchange_start(g)
 
         for s in range(splits):
-            begin = last + s * pairs
-
-            @pl.when((f >= begin) & (f < begin + pairs))
+            begin = last + s * tuples
+
+            @pl.when((f >= begin) & (f < begin + tuples))
             def _(s=s, begin=begin):
                 project_last(s, f - begin)
 
             if aligned and s < splits - 1:
 
-                @pl.when(f == begin + pairs - 1)
+                @pl.when(f == begin + tuples - 1)
                 def _(s=s):
                     exchange_start(groups - 1 + s)
 
     def near(h):
         return jnp.minimum(h, hcount - 1)
 
-    loads[2].wait()
+    kv_loads[0].wait()
     for c in fresh_local:
         c.wait()
     for c in fresh_remote[0]:
@@ -451,51 +501,53 @@
         math.log2(math.e) / HD**0.5
     )
     soften(0, 0)
-    loads[3].wait()
-    weigh(0, 0)
+    kv_loads[1].wait()
+    weigh(0, 0, 0)
     service(0)
+    loads[4].start()
     soften(min(1, hcount - 1), 1)
     scores(min(2, hcount - 1), 0)
 
+    unroll = max(splits, 2)
+
     def body(i, carry):
-        for u in range(2):
-            t = 2 * i + u
+        for u in range(unroll):
+            t = unroll * i + u
             if len(cuts) > 1:
 
                 @pl.when(t + 3 == ahead)
                 def _():
                     for c in fresh_remote[1]:
                         c.wait_recv()
+                    for c in kv_loads[2:]:
+                        c.wait()
 
             @pl.when(t + 1 < hcount)
             def _(t=t, u=u):
-                scores(near(t + 3), 1 - u)
-                soften(near(t + 2), u)
-                weigh(near(t + 1), 1 - u)
+                scores(near(t + 3), (u + 1) % 2)
+                soften(near(t + 2), u % 2)
+                weigh(t + 1, (u + 1) % 2, (u + 1) % splits)
 
             finish(t)
             service(t + 1)
         return carry
 
-    lax.fori_loop(0, (chunks + LAG * (n - 1) + 1) // 2, body, 0)
-
-    def drain(h, carry):
+    lax.fori_loop(0, -(-(chunks + LAG * (n - 1)) // unroll), body, 0)
+
+    def settle():
+        for d in range(1, seq_n):
+            for side in (0, 1):
+                fresh_wait(d, side, slice(0, width)).wait_send()
+        for c in sq_copies:
+            c.wait_send()
+
         @pl.when(z < n - 1)
         def _():
-            for c in send(h, 1):
-                c.wait_send()
+            settle_sends(1)
 
         @pl.when(z > 0)
         def _():
-            for c in send(h, -1):
-                c.wait_send()
-
-        return carry
-
-    def settle():
-        for c in [c for cut in fresh_remote for c in cut] + sq_copies:
-            c.wait_send()
-        lax.fori_loop(0, chunks, drain, 0)
+            settle_sends(-1)
 
     if aligned:
         cp = out_ref.shape[1]
@@ -508,9 +560,15 @@
                 c.wait_recv()
                 summed = summed + xr[d, a:b].astype(F32)
             out_ref[a:b, :] = (summed * gate[...]).astype(out_ref.dtype)
-        for k in range(len(pieces)):
-            for c in exchange(k):
-                c.wait_send()
+        for d in range(1, heads_n):
+            pltpu.make_async_remote_copy(
+                src_ref=xs.at[d - 1],
+                dst_ref=xr.at[d - 1],
+                send_sem=x_send.at[d - 1],
+                recv_sem=x_recv.at[d - 1, 0],
+                device_id={"head": lax.rem(hx + d, heads_n)},
+                device_id_type=MESH,
+            ).wait_send()
     else:
         out_ref[...] = acc[...]
         settle()
@@ -545,6 +603,7 @@
     xcount = max(heads_n - 1, 1)
     groups = rows // HD
     chunks = groups * hcount
+    ring = min(chunks, LAG * (n - 1) + 1)
     stat = (chunks, 2, HD)
     keys = cached + seq_n * 2 * fresh
     part = (chunks, HD, HD)
@@ -575,26 +634,28 @@
             pltpu.VMEM(stat, F32),
             pltpu.VMEM(part, BF16),
             pltpu.VMEM(stat, F32),
-            pltpu.VMEM((groups + 1, width, HD), BF16),
+            pltpu.VMEM((groups + SPLIT - 1, width, HD), BF16),
             pltpu.VMEM((rows, columns), F32),
             pltpu.VMEM((1, cp), F32),
             pltpu.VMEM((xcount, rows, cp), BF16),
             pltpu.VMEM((xcount, rows, cp), BF16),
             dma((6,)),
-            dma((4,)),
-            dma((max(seq_n - 1, 1), 2, 4)),
-            dma((max(seq_n - 1, 1), 2, 4)),
+            dma((2,)),
+            dma((max(seq_n - 1, 1), 2)),
+            dma((max(seq_n - 1, 1), 2, 2)),
             dma((xcount,)),
             dma((xcount,)),
-            dma((chunks, 2)),
-            dma((chunks, 2)),
-            dma((chunks, 2)),
-            dma((chunks, 2)),
-            dma((xcount, groups + 1)),
-            dma((xcount, groups + 1)),
+            dma((2,)),
+            dma((ring, 2)),
+            dma((2,)),
+            dma((ring, 2)),
+            dma((xcount,)),
+            dma((xcount, groups + SPLIT - 1)),
             pltpu.VMEM((2, keys, rows), F32),
             pltpu.VMEM((2, keys, rows), BF16),
             pltpu.VMEM((2, 4, rows), F32),
+            dma((PARTS,)),
+            dma((2, 2)),
         ],
         compiler_params=pltpu.CompilerParams(
             collective_id=0, has_side_effects=True, vmem_limit_bytes=60 * 1024 * 1024

time: 56 us -> 53.5 us (0.955)
  Pallas kernels: 53.8 us -> 51.3 us
    pallas_call x1, Pallas kernels: 53.8 us -> 51.3 us  [local(): pl.pallas_call(functools.partial(kernel, sizes, aligned), out_shape=pltpu...]
where the time goes in v3:
time: 53.5 us; the launch traced here: 53.3 us
  Pallas kernels  51.3 us (96%)
  between operations  1.3 us (2%)
  local copies, waits for them, and re-layouts  0.73 us (1%)
    pallas_call x1, Pallas kernels, local(): pl.pallas_call(functools.partial(kernel, sizes, aligned), out_shape=pltpu...  51.3 us

profile of v3, /device:TPU:0, one launch (start us, length us, event | category | flops | bytes accessed | tf_op | source)
XLA Modules:
  0.0 53.3 jit_solution(800642421219299477)
XLA Ops:
  1.3 51.3 %sweep_attention.1 = bf16[256,640]{1,0:T(8,128)(2,1)S(1)} custom-call(bf16[256,2560]{1,0:T(8,128)(2,1)} %q_ref.1, f32[2560]{0:T(1024)} %gain_ref.1, bf16[512,2560]{1,0:T(8,128)(2,1)} %ck_ref.1, bf16[512,2560]{1,0:T(8,128)(2,1)} %cv_ref.1, bf16[64,2560]{1,0:T(8,128)(2,1)} %fk_ref.1, bf16[64,2560]{1,0:T(8,128)(2,1)} %fv_ref.1, bf16[64,2560]{1,0:T(8,128)(2,1)} %nk_ref.1, ...), custom_call_target="tpu_custom_call" | custom-call | tf_op jit(solution)/shard_map/sweep_attention/pallas_call | solution.py:610
  52.6 0.7 %copy.14 = bf16[256,640]{1,0:T(8,128)(2,1)} copy(bf16[256,640]{1,0:T(8,128)(2,1)S(1)} %sweep_attention.1) | data formatting | bytes 655360

commit v4 on v3

--- a/solution.py
+++ b/solution.py
@@ -13,7 +13,7 @@
 EPSILON = 1e-06
 LOW = -1e30
 LAG = 5
-SPLIT = 4
+SPLIT = 2
 PARTS = 4
 MESH = pl.DeviceIdType.MESH
 F32 = jnp.float32
@@ -79,6 +79,7 @@
     m_buf,
     q_sem,
     kv_sem,
+    gauge,
 ):
     n, heads_n, seq_n = dims
     rows, width = q_ref.shape
@@ -89,11 +90,9 @@
 
     groups = rows // HD
     chunks = groups * hcount
-    loads = [
+    gain_load, w_load, tw_load = [
         pltpu.make_async_copy(src, dst, load_sem.at[i])
-        for i, (src, dst) in enumerate(
-            [(q_ref, q), (gain_ref, gain), (ck_ref, kc), (cv_ref, vc), (w_ref, w), (tw_ref, tw)]
-        )
+        for i, (src, dst) in enumerate([(gain_ref, gain), (w_ref, w), (tw_ref, tw)])
     ]
     ahead = min(max(hcount // 5, 3), hcount)
     parts = PARTS if hcount % PARTS == 0 else 1
@@ -106,7 +105,7 @@
     ]
     for c in q_loads:
         c.start()
-    loads[1].start()
+    gain_load.start()
     barrier = pltpu.get_barrier_semaphore()
     for d in range(1, seq_n):
         pl.semaphore_signal(
@@ -153,7 +152,7 @@
         for i, (src, dst) in enumerate([(ck_ref, kc), (cv_ref, vc)]):
             kv_loads.append(pltpu.make_async_copy(src.at[:, cols], dst.at[:, cols], kv_sem.at[k, i]))
     fresh_src = [(fk_ref, kf, 0), (nk_ref, kf, 1), (fv_ref, vf, 0), (nv_ref, vf, 1)]
-    loads[5].start()
+    tw_load.start()
     for c in kv_loads:
         c.start()
     fresh_local = []
@@ -162,7 +161,7 @@
     for side, whole in enumerate((kf, vf)):
         fresh_local.append(pltpu.make_async_copy(whole.at[sq], whole.at[sq], fresh_sem.at[side]))
     row_total = jnp.sum(total.T, axis=0, keepdims=True)
-    squares[hx] = jnp.broadcast_to(row_total, (8, rows))
+    squares[hx] = row_total
 
     ends = (z == 0).astype(jnp.int32) + (z == n - 1).astype(jnp.int32)
     pl.semaphore_wait(barrier, seq_n - 1 + heads_n - 1 + 2 - ends)
@@ -208,7 +207,7 @@
                 ).start()
             fresh_remote[k] += [fresh_wait(d, side, cols, k) for side in (0, 1)]
 
-    loads[1].wait()
+    gain_load.wait()
 
     def gain_step(h, carry):
         cols = pl.ds(pl.multiple_of(h * HD, HD), HD)
@@ -216,7 +215,7 @@
         return carry
 
     lax.fori_loop(0, hcount, gain_step, 0)
-    loads[5].wait()
+    tw_load.wait()
     if aligned:
         half = tw.shape[0] // 2
         j = lax.broadcasted_iota(jnp.int32, (half, HD), 0).astype(F32)
@@ -241,12 +240,23 @@
                 src_ref=src.at[h],
                 dst_ref=dst.at[h],
                 send_sem=ss.at[i],
-                recv_sem=rs.at[lax.rem(h, ring), i],
+                recv_sem=rs.at[lax.rem(h, ring)],
                 device_id={"slab": z + direction},
                 device_id_type=MESH,
             )
             for i, (src, dst) in enumerate(pairs)
         ]
+
+    def arrived(h, direction):
+        ss, rs = (right_send, right_recv) if direction > 0 else (left_send, left_recv)
+        pltpu.make_async_remote_copy(
+            src_ref=gauge,
+            dst_ref=gauge,
+            send_sem=ss.at[0],
+            recv_sem=rs.at[lax.rem(h, ring)],
+            device_id={"slab": z - direction},
+            device_id_type=MESH,
+        ).wait_recv()
 
     def settle_sends(direction):
         if direction > 0:
@@ -258,7 +268,7 @@
                 src_ref=src,
                 dst_ref=dst,
                 send_sem=ss.at[i],
-                recv_sem=rs.at[0, i],
+                recv_sem=rs.at[0],
                 device_id={"slab": z + direction},
                 device_id_type=MESH,
             ).wait_send()
@@ -309,17 +319,18 @@
         m_buf[slot, 0:1, :] = top
         m_buf[slot, 1:2, :] = jnp.max(part, axis=0, keepdims=True)
 
-    def soften(h, slot):
-        s_row = scale[0:1]
-        top = jnp.maximum(m_buf[slot, 0:1, :] * s_row + penalty, m_buf[slot, 1:2, :] * s_row)
-        top_c = top - penalty
-        mass = jnp.zeros((1, rows), F32)
+    def soften(slot, r=slice(None)):
+        s_row = scale[0:1, r]
+        mask = penalty[:, r]
+        top = jnp.maximum(m_buf[slot, 0:1, r] * s_row + mask, m_buf[slot, 1:2, r] * s_row)
+        top_c = top - mask
+        mass = jnp.zeros_like(top)
         for a, b in blocks + [(cached, cached + fresh_rows)]:
-            p = jnp.exp2(s_buf[slot, a:b, :] * s_row - (top_c if a < cached else top))
-            p_buf[slot, a:b, :] = p.astype(BF16)
+            p = jnp.exp2(s_buf[slot, a:b, r] * s_row - (top_c if a < cached else top))
+            p_buf[slot, a:b, r] = p.astype(BF16)
             mass = mass + jnp.sum(p, axis=0, keepdims=True)
-        m_buf[slot, 2:3, :] = top
-        m_buf[slot, 3:4, :] = mass
+        m_buf[slot, 2:3, r] = top
+        m_buf[slot, 3:4, r] = mass
 
     def place(g, h, seat, value, store):
         if g < groups - 1 or splits == 1:
@@ -330,25 +341,26 @@
             source = value if s == seat else pltpu.roll(value, (seat - s) % splits * sub, 1)
             store(last + s * tuples + lax.div(h, splits), lanes, source[:, lanes])
 
-    def weigh(h, slot, seat):
+    def weigh(h, slot, seat, first=0, end=None):
         cols = head_cols(h)
+        end = groups if end is None else end
+        r = slice(first * HD, end * HD)
         v_fresh = vf[:, :, :, cols].reshape(fresh_rows, HD)
-        o = lax.dot_general(v_fresh, p_buf[slot, cached:, :], tn, preferred_element_type=F32)
+        o = lax.dot_general(v_fresh, p_buf[slot, cached:, r], tn, preferred_element_type=F32)
         for a, b in blocks:
             o += lax.dot_general(
-                vc[a:b, cols], p_buf[slot, a:b, :], tn, preferred_element_type=F32
+                vc[a:b, cols], p_buf[slot, a:b, r], tn, preferred_element_type=F32
             )
-        for g in range(groups):
-            part = slice(g * HD, (g + 1) * HD)
-
-            def store_o(c, lanes, value):
-                own_o[c, :, lanes] = value
-
-            def store_s(c, lanes, value):
-                own_s[c, :, lanes] = value
-
-            place(g, h, seat, o[:, part], store_o)
-            place(g, h, seat, m_buf[slot, 2:4, part], store_s)
+
+        def store_o(c, lanes, value):
+            own_o[c, :, lanes] = value
+
+        def store_s(c, lanes, value):
+            own_s[c, :, lanes] = value
+
+        for g in range(first, end):
+            place(g, h, seat, o[:, (g - first) * HD : (g - first + 1) * HD], store_o)
+            place(g, h, seat, m_buf[slot, 2:4, g * HD : (g + 1) * HD], store_s)
 
     def project(g, p):
         deep = pl.ds(pl.multiple_of(p * pair * HD, HD), pair * HD)
@@ -407,8 +419,7 @@
 
         @pl.when(in_p & (z > 0))
         def _():
-            for c in send(cp_, 1):
-                c.wait_recv()
+            arrived(cp_, 1)
 
         @pl.when(in_p & (z < n - 1))
         def _():
@@ -418,8 +429,7 @@
 
         @pl.when(in_s & (z < n - 1))
         def _():
-            for c in send(cs, -1):
-                c.wait_recv()
+            arrived(cs, -1)
 
         @pl.when(in_s & (z > 0))
         def _():
@@ -456,7 +466,7 @@
 
         @pl.when(f == hcount - pairs)
         def _():
-            loads[4].wait()
+            w_load.wait()
 
         for g in range(groups - 1):
             begin = (g + 1) * hcount - pairs
@@ -474,7 +484,9 @@
         for s in range(splits):
             begin = last + s * tuples
 
-            @pl.when((f >= begin) & (f < begin + tuples))
+            stop = begin + tuples - (1 if aligned and s == splits - 1 else 0)
+
+            @pl.when((f >= begin) & (f < stop))
             def _(s=s, begin=begin):
                 project_last(s, f - begin)
 
@@ -483,6 +495,28 @@
                 @pl.when(f == begin + tuples - 1)
                 def _(s=s):
                     exchange_start(groups - 1 + s)
+
+        if aligned:
+
+            @pl.when(f == chunks - 1)
+            def _():
+                a, b = pieces[-1]
+                cp = out_ref.shape[1]
+                deep = slice((tuples - 1) * splits * HD, tuples * splits * HD)
+                sums = att[groups + splits - 2, deep, 0:sub]
+
+                def total_of(owner):
+                    cols = pl.ds(pl.multiple_of(owner * cp, HD), cp)
+                    before = 0.0 if tuples == 1 else acc[a:b, cols]
+                    return cols, before + lax.dot_general(
+                        sums, w[deep, cols], tn, preferred_element_type=F32
+                    )
+
+                for d, c in enumerate(exchange(len(pieces) - 1)):
+                    xs[d, a:b] = total_of(lax.rem(hx + d + 1, heads_n))[1].astype(BF16)
+                    c.start()
+                cols, own = total_of(hx)
+                acc[a:b, cols] = own
 
     def near(h):
         return jnp.minimum(h, hcount - 1)
@@ -500,12 +534,15 @@
     scale[...] = lax.rsqrt(norm_total / (HEADS * HD) + EPSILON) * (
         math.log2(math.e) / HD**0.5
     )
-    soften(0, 0)
+    soften(0, slice(0, HD))
     kv_loads[1].wait()
-    weigh(0, 0, 0)
+    weigh(0, 0, 0, 0, 1)
     service(0)
-    loads[4].start()
-    soften(min(1, hcount - 1), 1)
+    w_load.start()
+    if groups > 1:
+        soften(0, slice(HD, rows))
+        weigh(0, 0, 0, 1, groups)
+    soften(1)
     scores(min(2, hcount - 1), 0)
 
     unroll = max(splits, 2)
@@ -525,7 +562,7 @@
             @pl.when(t + 1 < hcount)
             def _(t=t, u=u):
                 scores(near(t + 3), (u + 1) % 2)
-                soften(near(t + 2), u % 2)
+                soften(u % 2)
                 weigh(t + 1, (u + 1) % 2, (u + 1) % splits)
 
             finish(t)
@@ -552,7 +589,6 @@
     if aligned:
         cp = out_ref.shape[1]
         mine = pl.ds(pl.multiple_of(hx * cp, HD), cp)
-        exchange_start(len(pieces) - 1)
         settle()
         for k, (a, b) in enumerate(pieces):
             summed = acc[a:b, mine]
@@ -622,8 +658,8 @@
             pltpu.VMEM((seq_n, 2, fresh, width), BF16),
             pltpu.VMEM((width, columns), BF16),
             pltpu.VMEM((freq, cp), F32),
-            pltpu.VMEM((heads_n, 8, rows), F32),
-            pltpu.VMEM((8, rows), F32),
+            pltpu.VMEM((heads_n, 1, rows), F32),
+            pltpu.VMEM((1, rows), F32),
             pltpu.VMEM(part, F32),
             pltpu.VMEM(stat, F32),
             pltpu.VMEM(part, BF16),
@@ -639,16 +675,16 @@
             pltpu.VMEM((1, cp), F32),
             pltpu.VMEM((xcount, rows, cp), BF16),
             pltpu.VMEM((xcount, rows, cp), BF16),
-            dma((6,)),
+            dma((3,)),
             dma((2,)),
             dma((max(seq_n - 1, 1), 2)),
             dma((max(seq_n - 1, 1), 2, 2)),
             dma((xcount,)),
             dma((xcount,)),
             dma((2,)),
-            dma((ring, 2)),
+            dma((ring,)),
             dma((2,)),
-            dma((ring, 2)),
+            dma((ring,)),
             dma((xcount,)),
             dma((xcount, groups + SPLIT - 1)),
             pltpu.VMEM((2, keys, rows), F32),
@@ -656,6 +692,7 @@
             pltpu.VMEM((2, 4, rows), F32),
             dma((PARTS,)),
             dma((2, 2)),
+            pltpu.VMEM((HD // 4 + 1, 2, HD), F32),
         ],
         compiler_params=pltpu.CompilerParams(
             collective_id=0, has_side_effects=True, vmem_limit_bytes=60 * 1024 * 1024

time: 53.5 us -> 52.7 us (0.985)
  Pallas kernels: 51.3 us -> 50.5 us
    pallas_call x1, Pallas kernels: 51.3 us -> 50.5 us  [local(): pl.pallas_call(functools.partial(kernel, sizes, aligned), out_shape=pltpu...]
where the time goes in v4:
time: 52.7 us; the launch traced here: 52.6 us
  Pallas kernels  50.5 us (96%)
  between operations  1.3 us (2%)
  local copies, waits for them, and re-layouts  0.73 us (1%)
    pallas_call x1, Pallas kernels, local(): pl.pallas_call(functools.partial(kernel, sizes, aligned), out_shape=pltpu...  50.5 us

profile of v4, /device:TPU:0, one launch (start us, length us, event | category | flops | bytes accessed | tf_op | source)
XLA Modules:
  0.0 52.6 jit_solution(13207841288724106133)
XLA Ops:
  1.3 50.5 %sweep_attention.1 = bf16[256,640]{1,0:T(8,128)(2,1)S(1)} custom-call(bf16[256,2560]{1,0:T(8,128)(2,1)} %q_ref.1, f32[2560]{0:T(1024)} %gain_ref.1, bf16[512,2560]{1,0:T(8,128)(2,1)} %ck_ref.1, bf16[512,2560]{1,0:T(8,128)(2,1)} %cv_ref.1, bf16[64,2560]{1,0:T(8,128)(2,1)} %fk_ref.1, bf16[64,2560]{1,0:T(8,128)(2,1)} %fv_ref.1, bf16[64,2560]{1,0:T(8,128)(2,1)} %nk_ref.1, ...), custom_call_target="tpu_custom_call" | custom-call | tf_op jit(solution)/shard_map/sweep_attention/pallas_call | solution.py:646
  51.8 0.7 %copy.14 = bf16[256,640]{1,0:T(8,128)(2,1)} copy(bf16[256,640]{1,0:T(8,128)(2,1)S(1)} %sweep_attention.1) | data formatting | bytes 655360

commit v5 on v4

--- a/solution.py
+++ b/solution.py
@@ -126,8 +126,7 @@
 
     def clear(o_ref, s_ref):
         o_ref[...] = jnp.zeros_like(o_ref)
-        s_ref[:, 0:1, :] = jnp.full((chunks, 1, HD), LOW, F32)
-        s_ref[:, 1:2, :] = jnp.zeros((chunks, 1, HD), F32)
+        s_ref[...] = jnp.full((chunks, 1, HD), LOW, F32)
 
     @pl.when(z == 0)
     def _():
@@ -153,13 +152,6 @@
             kv_loads.append(pltpu.make_async_copy(src.at[:, cols], dst.at[:, cols], kv_sem.at[k, i]))
     fresh_src = [(fk_ref, kf, 0), (nk_ref, kf, 1), (fv_ref, vf, 0), (nv_ref, vf, 1)]
     tw_load.start()
-    for c in kv_loads:
-        c.start()
-    fresh_local = []
-    for i, (src, dst, part) in enumerate(fresh_src):
-        pltpu.make_async_copy(src, dst.at[sq, part], fresh_sem.at[i // 2]).start()
-    for side, whole in enumerate((kf, vf)):
-        fresh_local.append(pltpu.make_async_copy(whole.at[sq], whole.at[sq], fresh_sem.at[side]))
     row_total = jnp.sum(total.T, axis=0, keepdims=True)
     squares[hx] = row_total
 
@@ -178,6 +170,14 @@
         )
         c.start()
         sq_copies.append(c)
+
+    for c in kv_loads:
+        c.start()
+    fresh_local = []
+    for i, (src, dst, part) in enumerate(fresh_src):
+        pltpu.make_async_copy(src, dst.at[sq, part], fresh_sem.at[i // 2]).start()
+    for side, whole in enumerate((kf, vf)):
+        fresh_local.append(pltpu.make_async_copy(whole.at[sq], whole.at[sq], fresh_sem.at[side]))
 
     edges = [0, ahead * HD, width] if ahead < hcount else [0, width]
     cuts = [slice(a, b) for a, b in zip(edges, edges[1:])]
@@ -283,13 +283,15 @@
     lag_end = LAG * jnp.maximum(z, n - 1 - z)
 
     def combine(h, other_o, other_s, dest_o, dest_s):
-        m_a, l_a = own_s[h, 0:1], own_s[h, 1:2]
-        m_b, l_b = other_s[h, 0:1], other_s[h, 1:2]
-        top = jnp.maximum(m_a, m_b)
-        e_a, e_b = jnp.exp2(m_a - top), jnp.exp2(m_b - top)
-        dest_o[h] = (own_o[h] * e_a + other_o[h].astype(F32) * e_b).astype(BF16)
-        dest_s[h, 0:1] = top
-        dest_s[h, 1:2] = l_a * e_a + l_b * e_b
+        l_a, l_b = own_s[h], other_s[h]
+        top = jnp.maximum(l_a, l_b)
+        e_a, e_b = jnp.exp2(l_a - top), jnp.exp2(l_b - top)
+        mass = e_a + e_b
+        share = 1.0 / mass
+        dest_o[h] = (
+            own_o[h] * (e_a * share) + other_o[h].astype(F32) * (e_b * share)
+        ).astype(BF16)
+        dest_s[h] = top + jnp.log2(mass)
 
     nt = (((1,), (1,)), ((), ()))
     tn = (((0,), (0,)), ((), ()))
@@ -329,8 +331,8 @@
             p = jnp.exp2(s_buf[slot, a:b, r] * s_row - (top_c if a < cached else top))
             p_buf[slot, a:b, r] = p.astype(BF16)
             mass = mass + jnp.sum(p, axis=0, keepdims=True)
-        m_buf[slot, 2:3, r] = top
-        m_buf[slot, 3:4, r] = mass
+        m_buf[slot, 2:3, r] = 1.0 / mass
+        m_buf[slot, 3:4, r] = top + jnp.log2(mass)
 
     def place(g, h, seat, value, store):
         if g < groups - 1 or splits == 1:
@@ -352,6 +354,8 @@
                 vc[a:b, cols], p_buf[slot, a:b, r], tn, preferred_element_type=F32
             )
 
+        o = o * m_buf[slot, 2:3, r]
+
         def store_o(c, lanes, value):
             own_o[c, :, lanes] = value
 
@@ -360,7 +364,7 @@
 
         for g in range(first, end):
             place(g, h, seat, o[:, (g - first) * HD : (g - first + 1) * HD], store_o)
-            place(g, h, seat, m_buf[slot, 2:4, g * HD : (g + 1) * HD], store_s)
+            place(g, h, seat, m_buf[slot, 3:4, g * HD : (g + 1) * HD], store_s)
 
     def project(g, p):
         deep = pl.ds(pl.multiple_of(p * pair * HD, HD), pair * HD)
@@ -442,14 +446,16 @@
 
         @pl.when((f >= 0) & (f < chunks))
         def _():
-            m_a, m_b, m_c = own_s[f, 0:1], pre_s[f, 0:1], suf_s[f, 0:1]
+            m_a, m_b, m_c = own_s[f], pre_s[f], suf_s[f]
             top = jnp.maximum(m_a, jnp.maximum(m_b, m_c))
             e_a, e_b, e_c = jnp.exp2(m_a - top), jnp.exp2(m_b - top), jnp.exp2(m_c - top)
-            mass = own_s[f, 1:2] * e_a + pre_s[f, 1:2] * e_b + suf_s[f, 1:2] * e_c
+            share = 1.0 / (e_a + e_b + e_c)
             total_o = (
-                own_o[f] * e_a + pre_o[f].astype(F32) * e_b + suf_o[f].astype(F32) * e_c
+                own_o[f] * (e_a * share)
+                + pre_o[f].astype(F32) * (e_b * share)
+                + suf_o[f].astype(F32) * (e_c * share)
             )
-            value = (total_o / mass).astype(BF16)
+            value = total_o.astype(BF16)
 
             @pl.when(f < last)
             def _():
@@ -461,7 +467,7 @@
                 k = f - last
                 s, p = lax.div(k, tuples), lax.rem(k, tuples)
                 for i in range(splits):
-                    turned = value if i == 0 else pltpu.roll(total_o / mass, HD - i * sub, 1).astype(BF16)
+                    turned = value if i == 0 else pltpu.roll(total_o, HD - i * sub, 1).astype(BF16)
                     att[groups - 1 + s, head_cols(p * splits + i), :] = turned
 
         @pl.when(f == hcount - pairs)
@@ -640,7 +646,7 @@
     groups = rows // HD
     chunks = groups * hcount
     ring = min(chunks, LAG * (n - 1) + 1)
-    stat = (chunks, 2, HD)
+    stat = (chunks, 1, HD)
     keys = cached + seq_n * 2 * fresh
     part = (chunks, HD, HD)
     result = pl.pallas_call(
@@ -692,7 +698,7 @@
             pltpu.VMEM((2, 4, rows), F32),
             dma((PARTS,)),
             dma((2, 2)),
-            pltpu.VMEM((HD // 4 + 1, 2, HD), F32),
+            pltpu.VMEM((HD // 2 + 1, 1, HD), F32),
         ],
         compiler_params=pltpu.CompilerParams(
             collective_id=0, has_side_effects=True, vmem_limit_bytes=60 * 1024 * 1024

time: 52.7 us -> 52.5 us (level)
  no operation moved by 1% of the time
where the time goes in v5:
time: 52.5 us; the launch traced here: 52.3 us
  Pallas kernels  50.3 us (96%)
  between operations  1.3 us (2%)
  local copies, waits for them, and re-layouts  0.73 us (1%)
    pallas_call x1, Pallas kernels, local(): pl.pallas_call(functools.partial(kernel, sizes, aligned), out_shape=pltpu...  50.3 us

profile of v5, /device:TPU:0, one launch (start us, length us, event | category | flops | bytes accessed | tf_op | source)
XLA Modules:
  0.0 52.3 jit_solution(5059243422955867065)
XLA Ops:
  1.3 50.3 %sweep_attention.1 = bf16[256,640]{1,0:T(8,128)(2,1)S(1)} custom-call(bf16[256,2560]{1,0:T(8,128)(2,1)} %q_ref.1, f32[2560]{0:T(1024)} %gain_ref.1, bf16[512,2560]{1,0:T(8,128)(2,1)} %ck_ref.1, bf16[512,2560]{1,0:T(8,128)(2,1)} %cv_ref.1, bf16[64,2560]{1,0:T(8,128)(2,1)} %fk_ref.1, bf16[64,2560]{1,0:T(8,128)(2,1)} %fv_ref.1, bf16[64,2560]{1,0:T(8,128)(2,1)} %nk_ref.1, ...), custom_call_target="tpu_custom_call" | custom-call | tf_op jit(solution)/shard_map/sweep_attention/pallas_call | solution.py:652
  51.6 0.7 %copy.14 = bf16[256,640]{1,0:T(8,128)(2,1)} copy(bf16[256,640]{1,0:T(8,128)(2,1)S(1)} %sweep_attention.1) | data formatting | bytes 655360

commit v6 on v5

--- a/solution.py
+++ b/solution.py
@@ -14,7 +14,7 @@
 LOW = -1e30
 LAG = 5
 SPLIT = 2
-PARTS = 4
+PARTS = 1
 MESH = pl.DeviceIdType.MESH
 F32 = jnp.float32
 BF16 = jnp.bfloat16
@@ -97,12 +97,13 @@
     ahead = min(max(hcount // 5, 3), hcount)
     parts = PARTS if hcount % PARTS == 0 else 1
     span = width // parts
-    q_loads = [
-        pltpu.make_async_copy(
-            q_ref.at[:, k * span : (k + 1) * span], q.at[:, k * span : (k + 1) * span], q_sem.at[k]
-        )
-        for k in range(parts)
-    ]
+    q_loads = []
+    for g in range(groups):
+        for k in range(parts):
+            at = (slice(g * HD, (g + 1) * HD), slice(k * span, (k + 1) * span))
+            q_loads.append(
+                pltpu.make_async_copy(q_ref.at[at], q.at[at], q_sem.at[g * parts + k])
+            )
     for c in q_loads:
         c.start()
     gain_load.start()
@@ -136,14 +137,20 @@
     def _():
         clear(suf_o, suf_s)
 
-    def squares_step(h, total):
-        x = q[:, pl.ds(pl.multiple_of(h * HD, HD), HD)].astype(F32)
-        return total + x * x
-
-    total = jnp.zeros((rows, HD), F32)
-    for k, c in enumerate(q_loads):
-        c.wait()
-        total = lax.fori_loop(k * hcount // parts, (k + 1) * hcount // parts, squares_step, total)
+    def squares_of(g):
+        def step(h, total):
+            x = q[g * HD : (g + 1) * HD, pl.ds(pl.multiple_of(h * HD, HD), HD)].astype(F32)
+            return total + x * x
+
+        total = jnp.zeros((HD, HD), F32)
+        for k in range(parts):
+            q_loads[g * parts + k].wait()
+            total = lax.fori_loop(
+                k * hcount // parts, (k + 1) * hcount // parts, step, total, unroll=True
+            )
+        squares[hx, g] = jnp.sum(total.T, axis=0, keepdims=True)
+
+    squares_of(0)
     head_cut = ahead * HD
     kv_cuts = [slice(0, head_cut), slice(head_cut, width)] if head_cut < width else [slice(0, width)]
     kv_loads = []
@@ -151,27 +158,35 @@
         for i, (src, dst) in enumerate([(ck_ref, kc), (cv_ref, vc)]):
             kv_loads.append(pltpu.make_async_copy(src.at[:, cols], dst.at[:, cols], kv_sem.at[k, i]))
     fresh_src = [(fk_ref, kf, 0), (nk_ref, kf, 1), (fv_ref, vf, 0), (nv_ref, vf, 1)]
-    tw_load.start()
-    row_total = jnp.sum(total.T, axis=0, keepdims=True)
-    squares[hx] = row_total
 
     ends = (z == 0).astype(jnp.int32) + (z == n - 1).astype(jnp.int32)
     pl.semaphore_wait(barrier, seq_n - 1 + heads_n - 1 + 2 - ends)
 
     sq_copies = []
-    for d in range(1, heads_n):
-        c = pltpu.make_async_remote_copy(
-            src_ref=squares.at[hx],
-            dst_ref=squares.at[hx],
-            send_sem=sq_send.at[d - 1],
-            recv_sem=sq_recv.at[d - 1],
-            device_id={"head": lax.rem(hx + d, heads_n)},
-            device_id_type=MESH,
-        )
+
+    def squares_send(g):
+        copies = []
+        for d in range(1, heads_n):
+            c = pltpu.make_async_remote_copy(
+                src_ref=squares.at[hx, g],
+                dst_ref=squares.at[hx, g],
+                send_sem=sq_send.at[d - 1, g],
+                recv_sem=sq_recv.at[d - 1, g],
+                device_id={"head": lax.rem(hx + d, heads_n)},
+                device_id_type=MESH,
+            )
+            c.start()
+            copies.append(c)
+        sq_copies.append(copies)
+
+    squares_send(0)
+    for c in kv_loads[:2]:
         c.start()
-        sq_copies.append(c)
-
-    for c in kv_loads:
+    for g in range(1, groups):
+        squares_of(g)
+        squares_send(g)
+    tw_load.start()
+    for c in kv_loads[2:]:
         c.start()
     fresh_local = []
     for i, (src, dst, part) in enumerate(fresh_src):
@@ -534,17 +549,24 @@
         c.wait_recv()
     scores(0, 0)
     scores(min(1, hcount - 1), 1)
-    for c in sq_copies:
-        c.wait_recv()
-    norm_total = jnp.sum(squares[...], axis=0)
-    scale[...] = lax.rsqrt(norm_total / (HEADS * HD) + EPSILON) * (
-        math.log2(math.e) / HD**0.5
-    )
+    def rescale(g):
+        for c in sq_copies[g]:
+            c.wait_recv()
+        norm_total = squares[0, g]
+        for d in range(1, heads_n):
+            norm_total = norm_total + squares[d, g]
+        scale[0:1, g * HD : (g + 1) * HD] = lax.rsqrt(norm_total / (HEADS * HD) + EPSILON) * (
+            math.log2(math.e) / HD**0.5
+        )
+
+    rescale(0)
     soften(0, slice(0, HD))
     kv_loads[1].wait()
     weigh(0, 0, 0, 0, 1)
     service(0)
     w_load.start()
+    for g in range(1, groups):
+        rescale(g)
     if groups > 1:
         soften(0, slice(HD, rows))
         weigh(0, 0, 0, 1, groups)
@@ -581,7 +603,7 @@
         for d in range(1, seq_n):
             for side in (0, 1):
                 fresh_wait(d, side, slice(0, width)).wait_send()
-        for c in sq_copies:
+        for c in [c for copies in sq_copies for c in copies]:
             c.wait_send()
 
         @pl.when(z < n - 1)
@@ -664,7 +686,7 @@
             pltpu.VMEM((seq_n, 2, fresh, width), BF16),
             pltpu.VMEM((width, columns), BF16),
             pltpu.VMEM((freq, cp), F32),
-            pltpu.VMEM((heads_n, 1, rows), F32),
+            pltpu.VMEM((heads_n, groups, 1, HD), F32),
             pltpu.VMEM((1, rows), F32),
             pltpu.VMEM(part, F32),
             pltpu.VMEM(stat, F32),
@@ -685,8 +707,8 @@
             dma((2,)),
             dma((max(seq_n - 1, 1), 2)),
             dma((max(seq_n - 1, 1), 2, 2)),
-            dma((xcount,)),
-            dma((xcount,)),
+            dma((xcount, groups)),
+            dma((xcount, groups)),
             dma((2,)),
             dma((ring,)),
             dma((2,)),
@@ -696,7 +718,7 @@
             pltpu.VMEM((2, keys, rows), F32),
             pltpu.VMEM((2, keys, rows), BF16),
             pltpu.VMEM((2, 4, rows), F32),
-            dma((PARTS,)),
+            dma((groups * PARTS,)),
             dma((2, 2)),
             pltpu.VMEM((HD // 2 + 1, 1, HD), F32),
         ],

time: 52.5 us -> 52.4 us (level)
  no operation moved by 1% of the time
where the time goes in v6:
time: 52.4 us; the launch traced here: 52.2 us
  Pallas kernels  50.2 us (96%)
  between operations  1.3 us (2%)
  local copies, waits for them, and re-layouts  0.73 us (1%)
    pallas_call x1, Pallas kernels, local(): pl.pallas_call(functools.partial(kernel, sizes, aligned), out_shape=pltpu...  50.2 us

profile of v6, /device:TPU:0, one launch (start us, length us, event | category | flops | bytes accessed | tf_op | source)
XLA Modules:
  0.0 52.2 jit_solution(14306889801040902990)
XLA Ops:
  1.3 50.2 %sweep_attention.1 = bf16[256,640]{1,0:T(8,128)(2,1)S(1)} custom-call(bf16[256,2560]{1,0:T(8,128)(2,1)} %q_ref.1, f32[2560]{0:T(1024)} %gain_ref.1, bf16[512,2560]{1,0:T(8,128)(2,1)} %ck_ref.1, bf16[512,2560]{1,0:T(8,128)(2,1)} %cv_ref.1, bf16[64,2560]{1,0:T(8,128)(2,1)} %fk_ref.1, bf16[64,2560]{1,0:T(8,128)(2,1)} %fv_ref.1, bf16[64,2560]{1,0:T(8,128)(2,1)} %nk_ref.1, ...), custom_call_target="tpu_custom_call" | custom-call | tf_op jit(solution)/shard_map/sweep_attention/pallas_call | solution.py:674
  51.5 0.7 %copy.14 = bf16[256,640]{1,0:T(8,128)(2,1)} copy(bf16[256,640]{1,0:T(8,128)(2,1)S(1)} %sweep_attention.1) | data formatting | bytes 655360

commit v7 on v6

--- a/solution.py
+++ b/solution.py
@@ -33,8 +33,8 @@
     nv_ref,
     w_ref,
     tw_ref,
-    owner_ref,
-    step_ref,
+    owner_hbm,
+    step_hbm,
     out_ref,
     q,
     qg,
@@ -80,6 +80,11 @@
     q_sem,
     kv_sem,
     gauge,
+    raw_o,
+    raw_s,
+    owner_ref,
+    step_ref,
+    scalar_sem,
 ):
     n, heads_n, seq_n = dims
     rows, width = q_ref.shape
@@ -107,6 +112,12 @@
     for c in q_loads:
         c.start()
     gain_load.start()
+    scalars = [
+        pltpu.make_async_copy(owner_hbm, owner_ref, scalar_sem.at[0]),
+        pltpu.make_async_copy(step_hbm, step_ref, scalar_sem.at[1]),
+    ]
+    for c in scalars:
+        c.start()
     barrier = pltpu.get_barrier_semaphore()
     for d in range(1, seq_n):
         pl.semaphore_signal(
@@ -231,11 +242,13 @@
 
     lax.fori_loop(0, hcount, gain_step, 0)
     tw_load.wait()
+    for c in scalars:
+        c.wait()
     if aligned:
         half = tw.shape[0] // 2
         j = lax.broadcasted_iota(jnp.int32, (half, HD), 0).astype(F32)
         frequency = jnp.exp(F32(-math.log(10000.0)) * j / half)
-        phases = jnp.full((half, HD), step_ref[0], jnp.int32).astype(F32) * frequency
+        phases = jnp.full((half, HD), step_ref[0, 0], jnp.int32).astype(F32) * frequency
         cos, sin = jnp.cos(phases), jnp.sin(phases)
         for c in range(tw.shape[1] // HD):
             cols = slice(c * HD, (c + 1) * HD)
@@ -312,7 +325,7 @@
     tn = (((0,), (0,)), ((), ()))
 
     penalty = jnp.where(
-        jnp.full((1, rows), owner_ref[0], jnp.int32) == z, F32(LOW), F32(0.0)
+        jnp.full((1, rows), owner_ref[0, 0], jnp.int32) == z, F32(LOW), F32(0.0)
     )
     cached = kc.shape[0]
     step_keys = 256 if cached % 256 == 0 else cached
@@ -349,16 +362,22 @@
         m_buf[slot, 2:3, r] = 1.0 / mass
         m_buf[slot, 3:4, r] = top + jnp.log2(mass)
 
-    def place(g, h, seat, value, store):
-        if g < groups - 1 or splits == 1:
-            store(g * hcount + h, slice(0, HD), value)
-            return
-        lanes = slice(seat * sub, (seat + 1) * sub)
-        for s in range(splits):
-            source = value if s == seat else pltpu.roll(value, (seat - s) % splits * sub, 1)
-            store(last + s * tuples + lax.div(h, splits), lanes, source[:, lanes])
-
-    def weigh(h, slot, seat, first=0, end=None):
+    packed = splits > 1
+
+    def pack(c):
+        k = c - last
+        s, p = lax.div(k, tuples), lax.rem(k, tuples)
+        seat_o = lax.broadcasted_iota(jnp.int32, (HD, HD), 1) // sub
+        seat_s = lax.broadcasted_iota(jnp.int32, (1, HD), 1) // sub
+        value, stats = jnp.zeros((HD, HD), F32), jnp.zeros((1, HD), F32)
+        for i in range(splits):
+            turn = lax.rem((i - s + splits) * sub, HD)
+            value = jnp.where(seat_o == i, pltpu.roll(raw_o[p * splits + i], turn, 1), value)
+            stats = jnp.where(seat_s == i, pltpu.roll(raw_s[p * splits + i], turn, 1), stats)
+        own_o[c] = value
+        own_s[c] = stats
+
+    def weigh(h, slot, first=0, end=None):
         cols = head_cols(h)
         end = groups if end is None else end
         r = slice(first * HD, end * HD)
@@ -371,15 +390,12 @@
 
         o = o * m_buf[slot, 2:3, r]
 
-        def store_o(c, lanes, value):
-            own_o[c, :, lanes] = value
-
-        def store_s(c, lanes, value):
-            own_s[c, :, lanes] = value
-
         for g in range(first, end):
-            place(g, h, seat, o[:, (g - first) * HD : (g - first + 1) * HD], store_o)
-            place(g, h, seat, m_buf[slot, 3:4, g * HD : (g + 1) * HD], store_s)
+            to_o, to_s, at = own_o, own_s, g * hcount + h
+            if packed and g == groups - 1:
+                to_o, to_s, at = raw_o, raw_s, h
+            to_o[at] = o[:, (g - first) * HD : (g - first + 1) * HD]
+            to_s[at] = m_buf[slot, 3:4, g * HD : (g + 1) * HD]
 
     def project(g, p):
         deep = pl.ds(pl.multiple_of(p * pair * HD, HD), pair * HD)
@@ -562,18 +578,18 @@
     rescale(0)
     soften(0, slice(0, HD))
     kv_loads[1].wait()
-    weigh(0, 0, 0, 0, 1)
+    weigh(0, 0, 0, 1)
     service(0)
     w_load.start()
     for g in range(1, groups):
         rescale(g)
     if groups > 1:
         soften(0, slice(HD, rows))
-        weigh(0, 0, 0, 1, groups)
+        weigh(0, 0, 1, groups)
     soften(1)
     scores(min(2, hcount - 1), 0)
 
-    unroll = max(splits, 2)
+    unroll = 2
 
     def body(i, carry):
         for u in range(unroll):
@@ -591,7 +607,14 @@
             def _(t=t, u=u):
                 scores(near(t + 3), (u + 1) % 2)
                 soften(u % 2)
-                weigh(t + 1, (u + 1) % 2, (u + 1) % splits)
+                weigh(t + 1, (u + 1) % 2)
+
+            if packed:
+                c = t + 1 + tuples
+
+                @pl.when((c >= last) & (c < chunks))
+                def _(c=c):
+                    pack(c)
 
             finish(t)
             service(t + 1)
@@ -661,7 +684,6 @@
     freq = time_weight.shape[0]
     aligned = cp % HD == 0
     any_spec = pl.BlockSpec(memory_space=pl.ANY)
-    smem = pl.BlockSpec(memory_space=pltpu.SMEM)
     vmem = pl.BlockSpec(memory_space=pltpu.VMEM)
     dma = pltpu.SemaphoreType.DMA
     xcount = max(heads_n - 1, 1)
@@ -674,7 +696,7 @@
     result = pl.pallas_call(
         functools.partial(kernel, sizes, aligned),
         out_shape=pltpu.VMEM((rows, cp), BF16) if aligned else jax.ShapeDtypeStruct((rows, columns), F32),
-        in_specs=[any_spec] * 10 + [smem] * 2,
+        in_specs=[any_spec] * 12,
         out_specs=vmem,
         scratch_shapes=[
             pltpu.VMEM((rows, width), BF16),
@@ -721,6 +743,11 @@
             dma((groups * PARTS,)),
             dma((2, 2)),
             pltpu.VMEM((HD // 2 + 1, 1, HD), F32),
+            pltpu.VMEM((hcount, HD, HD), F32),
+            pltpu.VMEM((hcount, 1, HD), F32),
+            pltpu.SMEM((1, 1), jnp.int32),
+            pltpu.SMEM((1, 1), jnp.int32),
+            dma((2,)),
         ],
         compiler_params=pltpu.CompilerParams(
             collective_id=0, has_side_effects=True, vmem_limit_bytes=60 * 1024 * 1024
@@ -745,7 +772,7 @@
     summed = lax.psum_scatter(result, "head", scatter_dimension=1, tiled=True)
     half = freq // 2
     frequency = jnp.exp(-jnp.log(10000.0) * jnp.arange(half, dtype=F32) / half)
-    phases = step[0].astype(F32) * frequency
+    phases = step[0, 0].astype(F32) * frequency
     embedding = jnp.concatenate([jnp.cos(phases), jnp.sin(phases)])
     time_gate = 1.0 + jnp.dot(embedding, time_weight, precision=lax.Precision.HIGHEST)
     return (time_gate * summed).astype(BF16)
@@ -763,15 +790,20 @@
         P(("grp", "slab", "seq"), "head"),
         P("head", "slab"),
         P(None, ("slab", "head")),
-        P("grp"),
-        P("grp"),
+        P("grp", None),
+        P("grp", None),
     )
     out_specs = P(("grp", "seq"), ("slab", "head"))
     sizes = (mesh.shape["slab"], mesh.shape["head"], mesh.shape["seq"])
-    return jax.shard_map(
+    mapped = jax.shard_map(
         functools.partial(local, sizes),
         mesh=mesh,
         in_specs=in_specs,
         out_specs=out_specs,
         check_vma=False,
     )
+
+    def run(*args):
+        return mapped(*args[:-2], args[-2].reshape(-1, 1), args[-1].reshape(-1, 1))
+
+    return run

time: 52.4 us -> 52.4 us (level)
  no operation moved by 1% of the time
where the time goes in v7:
time: 52.4 us; the launch traced here: 52.3 us
  Pallas kernels  50.3 us (96%)
  between operations  1.3 us (2%)
  local copies, waits for them, and re-layouts  0.73 us (1%)
    pallas_call x1, Pallas kernels, local(): pl.pallas_call(functools.partial(kernel, sizes, aligned), out_shape=pltpu...  50.3 us

profile of v7, /device:TPU:0, one launch (start us, length us, event | category | flops | bytes accessed | tf_op | source)
XLA Modules:
  0.0 52.3 jit_solution(5436022059485247645)
XLA Ops:
  1.3 50.3 %sweep_attention.1 = bf16[256,640]{1,0:T(8,128)(2,1)S(1)} custom-call(bf16[256,2560]{1,0:T(8,128)(2,1)} %q_ref.1, f32[2560]{0:T(1024)} %gain_ref.1, bf16[512,2560]{1,0:T(8,128)(2,1)} %ck_ref.1, bf16[512,2560]{1,0:T(8,128)(2,1)} %cv_ref.1, bf16[64,2560]{1,0:T(8,128)(2,1)} %fk_ref.1, bf16[64,2560]{1,0:T(8,128)(2,1)} %fv_ref.1, bf16[64,2560]{1,0:T(8,128)(2,1)} %nk_ref.1, ...), custom_call_target="tpu_custom_call" | custom-call | tf_op jit(solution)/shard_map/sweep_attention/pallas_call | solution.py:696
  51.6 0.7 %copy.14 = bf16[256,640]{1,0:T(8,128)(2,1)} copy(bf16[256,640]{1,0:T(8,128)(2,1)S(1)} %sweep_attention.1) | data formatting | bytes 655360

commit v8 on v7

--- a/solution.py
+++ b/solution.py
@@ -459,7 +459,7 @@
         @pl.when(in_p & (z < n - 1))
         def _():
             combine(cp_, pre_o, pre_s, right_o, right_s)
-            for c in send(cp_, 1):
+            for c in send(cp_, 1)[::-1]:
                 c.start()
 
         @pl.when(in_s & (z < n - 1))
@@ -469,7 +469,7 @@
         @pl.when(in_s & (z > 0))
         def _():
             combine(cs, suf_o, suf_s, left_o, left_s)
-            for c in send(cs, -1):
+            for c in send(cs, -1)[::-1]:
                 c.start()
 
     def finish(t):

time: 52.4 us -> 52.2 us (level)
  no operation moved by 1% of the time
where the time goes in v8:
time: 52.2 us; the launch traced here: 52 us
  Pallas kernels  50 us (96%)
  between operations  1.3 us (2%)
  local copies, waits for them, and re-layouts  0.73 us (1%)
    pallas_call x1, Pallas kernels, local(): pl.pallas_call(functools.partial(kernel, sizes, aligned), out_shape=pltpu...  50 us

profile of v8, /device:TPU:0, one launch (start us, length us, event | category | flops | bytes accessed | tf_op | source)
XLA Modules:
  0.0 52.0 jit_solution(4904486342032835254)
XLA Ops:
  1.3 50.0 %sweep_attention.1 = bf16[256,640]{1,0:T(8,128)(2,1)S(1)} custom-call(bf16[256,2560]{1,0:T(8,128)(2,1)} %q_ref.1, f32[2560]{0:T(1024)} %gain_ref.1, bf16[512,2560]{1,0:T(8,128)(2,1)} %ck_ref.1, bf16[512,2560]{1,0:T(8,128)(2,1)} %cv_ref.1, bf16[64,2560]{1,0:T(8,128)(2,1)} %fk_ref.1, bf16[64,2560]{1,0:T(8,128)(2,1)} %fv_ref.1, bf16[64,2560]{1,0:T(8,128)(2,1)} %nk_ref.1, ...), custom_call_target="tpu_custom_call" | custom-call | tf_op jit(solution)/shard_map/sweep_attention/pallas_call | solution.py:696
  51.3 0.7 %copy.14 = bf16[256,640]{1,0:T(8,128)(2,1)} copy(bf16[256,640]{1,0:T(8,128)(2,1)S(1)} %sweep_attention.1) | data formatting | bytes 655360

commit v9 on v8

--- a/solution.py
+++ b/solution.py
@@ -581,12 +581,17 @@
     weigh(0, 0, 0, 1)
     service(0)
     w_load.start()
+    early = hcount > 1 and groups > 1
+    if early:
+        soften(1, slice(0, HD))
+        weigh(1, 1, 0, 1)
+        service(1)
     for g in range(1, groups):
         rescale(g)
     if groups > 1:
         soften(0, slice(HD, rows))
         weigh(0, 0, 1, groups)
-    soften(1)
+    soften(1, slice(HD, rows) if early else slice(None))
     scores(min(2, hcount - 1), 0)
 
     unroll = 2
@@ -617,7 +622,14 @@
                     pack(c)
 
             finish(t)
-            service(t + 1)
+            if early and u == 0:
+
+                @pl.when(t > 0)
+                def _(t=t):
+                    service(t + 1)
+
+            else:
+                service(t + 1)
         return carry
 
     lax.fori_loop(0, -(-(chunks + LAG * (n - 1)) // unroll), body, 0)

time: 52.2 us -> 52 us (level)
  no operation moved by 1% of the time
where the time goes in v9:
time: 52 us; the launch traced here: 51.9 us
  Pallas kernels  49.8 us (96%)
  between operations  1.3 us (2%)
  local copies, waits for them, and re-layouts  0.73 us (1%)
    pallas_call x1, Pallas kernels, local(): pl.pallas_call(functools.partial(kernel, sizes, aligned), out_shape=pltpu...  49.8 us

profile of v9, /device:TPU:0, one launch (start us, length us, event | category | flops | bytes accessed | tf_op | source)
XLA Modules:
  0.0 51.9 jit_solution(6269191401174897261)
XLA Ops:
  1.3 49.8 %sweep_attention.1 = bf16[256,640]{1,0:T(8,128)(2,1)S(1)} custom-call(bf16[256,2560]{1,0:T(8,128)(2,1)} %q_ref.1, f32[2560]{0:T(1024)} %gain_ref.1, bf16[512,2560]{1,0:T(8,128)(2,1)} %ck_ref.1, bf16[512,2560]{1,0:T(8,128)(2,1)} %cv_ref.1, bf16[64,2560]{1,0:T(8,128)(2,1)} %fk_ref.1, bf16[64,2560]{1,0:T(8,128)(2,1)} %fv_ref.1, bf16[64,2560]{1,0:T(8,128)(2,1)} %nk_ref.1, ...), custom_call_target="tpu_custom_call" | custom-call | tf_op jit(solution)/shard_map/sweep_attention/pallas_call | solution.py:708
  51.1 0.7 %copy.14 = bf16[256,640]{1,0:T(8,128)(2,1)} copy(bf16[256,640]{1,0:T(8,128)(2,1)S(1)} %sweep_attention.1) | data formatting | bytes 655360

commit v10 on v9

--- a/solution.py
+++ b/solution.py
@@ -452,6 +452,16 @@
         cs = t - LAG * (n - 1 - z)
         in_s = (cs >= 0) & (cs < chunks)
 
+        @pl.when(in_s & (z < n - 1))
+        def _():
+            arrived(cs, -1)
+
+        @pl.when(in_s & (z > 0))
+        def _():
+            combine(cs, suf_o, suf_s, left_o, left_s)
+            for c in send(cs, -1)[::-1]:
+                c.start()
+
         @pl.when(in_p & (z > 0))
         def _():
             arrived(cp_, 1)
@@ -460,16 +470,6 @@
         def _():
             combine(cp_, pre_o, pre_s, right_o, right_s)
             for c in send(cp_, 1)[::-1]:
-                c.start()
-
-        @pl.when(in_s & (z < n - 1))
-        def _():
-            arrived(cs, -1)
-
-        @pl.when(in_s & (z > 0))
-        def _():
-            combine(cs, suf_o, suf_s, left_o, left_s)
-            for c in send(cs, -1)[::-1]:
                 c.start()
 
     def finish(t):

time: 52 us -> 52 us (level)
  no operation moved by 1% of the time
where the time goes in v10:
time: 52 us; the launch traced here: 51.9 us
  Pallas kernels  49.8 us (96%)
  between operations  1.3 us (2%)
  local copies, waits for them, and re-layouts  0.73 us (1%)
    pallas_call x1, Pallas kernels, local(): pl.pallas_call(functools.partial(kernel, sizes, aligned), out_shape=pltpu...  49.8 us

profile of v10, /device:TPU:0, one launch (start us, length us, event | category | flops | bytes accessed | tf_op | source)
XLA Modules:
  0.0 51.9 jit_solution(14565878334436784145)
XLA Ops:
  1.3 49.8 %sweep_attention.1 = bf16[256,640]{1,0:T(8,128)(2,1)S(1)} custom-call(bf16[256,2560]{1,0:T(8,128)(2,1)} %q_ref.1, f32[2560]{0:T(1024)} %gain_ref.1, bf16[512,2560]{1,0:T(8,128)(2,1)} %ck_ref.1, bf16[512,2560]{1,0:T(8,128)(2,1)} %cv_ref.1, bf16[64,2560]{1,0:T(8,128)(2,1)} %fk_ref.1, bf16[64,2560]{1,0:T(8,128)(2,1)} %fv_ref.1, bf16[64,2560]{1,0:T(8,128)(2,1)} %nk_ref.1, ...), custom_call_target="tpu_custom_call" | custom-call | tf_op jit(solution)/shard_map/sweep_attention/pallas_call | solution.py:708
  51.2 0.7 %copy.14 = bf16[256,640]{1,0:T(8,128)(2,1)} copy(bf16[256,640]{1,0:T(8,128)(2,1)S(1)} %sweep_attention.1) | data formatting | bytes 655360
